TPU v7x, 256 devices: a whole 4x4x8 slice. The times are simulated.
256 devices in a mesh: py: 32 (over z, x), px: 8 (over y, core).
Axes of the slice: x: 4, y: 4, z: 8, core: 2. Of those that a mesh axis runs over, the one named last changes fastest.
Arguments:
- density: float32 [1024, 256, 128], P('py', 'px'), may hold values from 0.5 to 2
- conductance: float32 [1024, 256, 128], P('py', 'px'), may hold values from 0.03 to 0.22
- source: float32 [1024, 256, 128], P('py', 'px'), may hold values from -0.2 to 0.2
Outputs:
- anomaly: float32 [1024, 256, 128], P('py', 'px')
- density_end: float32 [1024, 256, 128], P('py', 'px')
All inputs are finite; a program needn't handle non-finite values.
Results may differ from a plain program's by a relative error of at most 0.00002.
Values sent between devices are 32-bit elements; how exact they have to be, the bound alone decides.
A program may use at most 64 MiB of HBM per device.

v0:
```python
import jax
import jax.numpy as jnp
from jax import lax
from jax.sharding import PartitionSpec as P

STEPS = 6


def with_halo(cells, sides, width):
    for axis, dim in sides:
        count = lax.axis_size(axis)
        ends = count - 1
        head = lax.slice_in_dim(cells, 0, width, axis=dim)
        tail = lax.slice_in_dim(cells, cells.shape[dim] - width, cells.shape[dim], axis=dim)
        cells = jnp.concatenate(
            [
                lax.ppermute(tail, axis, [(i, (i + 1) % count) for i in range(ends)]),
                cells,
                lax.ppermute(head, axis, [((i + 1) % count, i) for i in range(ends)]),
            ],
            axis=dim,
        )
    return cells


def sent_to_all(shard, axis):
    length = lax.axis_size(axis)
    return lax.all_to_all(
        jnp.broadcast_to(shard[None], (length, *shard.shape)), axis, 0, 0, tiled=True
    )


def over_copies(shard, axis):
    return sent_to_all(shard, axis).sum(axis=0)


def in_one(arrays, axis):
    ends = [0]
    for a in arrays:
        ends.append(ends[-1] + a.size)
    running = over_copies(jnp.concatenate([a.ravel() for a in arrays]), axis)
    return tuple((running[b:e].reshape(a.shape) for a, b, e in zip(arrays, ends, ends[1:])))


def strip_edges(values, dims):
    for dim in dims:
        values = lax.slice_in_dim(values, 1, values.shape[dim] - 1, axis=dim)
    return values


def neighbour(values, dim, start, dims):
    others = [other for other in dims if other != dim]
    values = strip_edges(values, others)
    return lax.slice_in_dim(values, start, start + values.shape[dim] - 2, axis=dim)


def one_step(padded, conductance, source):
    middle = strip_edges(padded, (0, 1))
    lower = [neighbour(padded, dim, 0, (0, 1)) for dim in (0, 1)]
    upper = [neighbour(padded, dim, 2, (0, 1)) for dim in (0, 1)]
    spread = lower[0] + upper[0] + lower[1] + upper[1] - 4.0 * middle
    return middle + conductance * spread + source


def per_device(density, conductance, source):
    padded = with_halo(density, (("py", 0), ("px", 1)), STEPS)
    wide_parts = with_halo(
        jnp.concatenate([conductance, source], axis=2), (("py", 0), ("px", 1)), STEPS - 1
    )
    wide_conductance, wide_source = jnp.split(wide_parts, 2, axis=2)
    for step in range(STEPS):
        later = one_step(padded, wide_conductance, wide_source)
        values = later
        margin = STEPS - 1 - step
        place = lax.axis_index("py") * density.shape[0] - margin + jnp.arange(values.shape[0])
        keep_cells = (place >= 0) & (place < density.shape[0] * lax.axis_size("py"))
        values = jnp.where(keep_cells.reshape((-1,) + (1,) * 2), values, 0.0)
        place = lax.axis_index("px") * density.shape[1] - margin + jnp.arange(values.shape[1])
        keep_cells = (place >= 0) & (place < density.shape[1] * lax.axis_size("px"))
        values = jnp.where(keep_cells.reshape((-1,) + (1,) * 1), values, 0.0)
        later = values
        if step < STEPS - 1:
            wide_conductance = strip_edges(wide_conductance, (0, 1))
            wide_source = strip_edges(wide_source, (0, 1))
        padded = later
    density = padded
    count = density.shape[0] * lax.axis_size("py")
    guess = 1.0
    moved = density - guess
    totals, squares = in_one(
        (jnp.sum(moved, axis=0, keepdims=True), jnp.sum(moved * moved, axis=0, keepdims=True)), "py"
    )
    line_mean = guess + totals / count
    centred = density - line_mean
    line_variance = squares / count - totals / count * (totals / count)
    anomaly = centred * lax.rsqrt(line_variance + 0.0001)
    return (anomaly, density)


def solution(mesh):
    in_specs = (P("py", "px", None), P("py", "px", None), P("py", "px", None))
    out_specs = (P("py", "px", None), P("py", "px", None))
    return jax.shard_map(
        per_device, mesh=mesh, in_specs=in_specs, out_specs=out_specs, check_vma=False
    )
```

profile of v0, /device:TPU:8, one launch (start us, length us, event | category | flops | bytes accessed | tf_op | source)
XLA Modules:
  0.0 82.5 jit_solution(9092601816657384523)
XLA Ops:
  0.6 1.1 %constant_dynamic-update-slice_fusion.4 = f32[32,32,256]{2,1,0:T(8,128)S(1)} fusion(f32[32,32,128]{2,1,0:T(8,128)} %param.4), kind=kLoop, calls=%fused_computation.74 | loop fusion | bytes 1048576
  1.8 1.1 %constant_dynamic-update-slice_fusion.3 = f32[32,32,256]{2,1,0:T(8,128)S(1)} fusion(f32[32,32,256]{2,1,0:T(8,128)S(1)} %constant_dynamic-update-slice_fusion.4, f32[32,32,128]{2,1,0:T(8,128)} %param.5), kind=kLoop, calls=%fused_computation.73 | loop fusion | bytes 1048576 | tf_op jit(solution)/shard_map/concatenate | solution.py:68
  2.9 1.3 %collective-permute-start.5 = (f32[5,32,256]{2,1,0:T(8,128)S(1)}, f32[5,32,256]{2,1,0:T(8,128)S(1)}, u32[]{:S(2)}, u32[]{:S(2)}) collective-permute-start(f32[5,32,256]{2,1,0:T(8,128)S(1)} %get-tuple-element.8), channel_id=1, source_target_pairs={{8,0},{16,8},{24,16},{32,24},{40,32},{48,40},{56,48},{64,56},{72,6... | collective-permute-start | bytes 491528 | tf_op jit(solution)/shard_map/ppermute | solution.py:19
  4.2 4.6 %collective-permute-start.4 = (f32[5,32,256]{2,1,0:T(8,128)S(1)}, f32[5,32,256]{2,1,0:T(8,128)S(1)}, u32[]{:S(2)}, u32[]{:S(2)}) collective-permute-start(f32[5,32,256]{2,1,0:T(8,128)S(1)} %get-tuple-element.7), channel_id=1, source_target_pairs={{0,8},{8,16},{16,24},{24,32},{32,40},{40,48},{48,56},{56,64},{64,7... | collective-permute-start | bytes 491528 | tf_op jit(solution)/shard_map/ppermute | solution.py:17
  8.8 3.4 %collective-permute-start = (f32[6,32,128]{2,1,0:T(8,128)S(1)}, f32[6,32,128]{2,1,0:T(8,128)S(1)}, u32[]{:S(2)}, u32[]{:S(2)}) collective-permute-start(f32[6,32,128]{2,1,0:T(8,128)S(1)} %get-tuple-element.12), channel_id=1, source_target_pairs={{0,8},{8,16},{16,24},{24,32},{32,40},{40,48},{48,56},{56,64},{64,7... | collective-permute-start | bytes 294920 | tf_op jit(solution)/shard_map/ppermute | solution.py:17
  12.2 1.3 %collective-permute-start.1 = (f32[6,32,128]{2,1,0:T(8,128)S(1)}, f32[6,32,128]{2,1,0:T(8,128)S(1)}, u32[]{:S(2)}, u32[]{:S(2)}) collective-permute-start(f32[6,32,128]{2,1,0:T(8,128)S(1)} %get-tuple-element.11), channel_id=1, source_target_pairs={{8,0},{16,8},{24,16},{32,24},{40,32},{48,40},{56,48},{64,56},{72,6... | collective-permute-start | bytes 294920 | tf_op jit(solution)/shard_map/ppermute | solution.py:19
  13.6 0.8 collective-permute-done
  14.4 4.3 %collective-permute-done.1 = f32[6,32,128]{2,1,0:T(8,128)S(1)} collective-permute-done((f32[6,32,128]{2,1,0:T(8,128)S(1)}, f32[6,32,128]{2,1,0:T(8,128)S(1)}, u32[]{:S(2)}, u32[]{:S(2)}) %collective-permute-start.1) | collective-permute-done | bytes 98336 | tf_op jit(solution)/shard_map/ppermute | solution.py:19
  18.8 1.9 %collective-permute-start.3 = (f32[44,6,128]{2,1,0:T(8,128)S(1)}, f32[44,6,128]{2,1,0:T(8,128)S(1)}, u32[]{:S(2)}, u32[]{:S(2)}) collective-permute-start(f32[44,6,128]{2,1,0:T(8,128)S(1)} %get-tuple-element.10), channel_id=1, source_target_pairs={{1,0},{2,1},{3,2},{4,3},{5,4},{6,5},{7,6},{9,8},{10,9},{11,10},{12... | collective-permute-start | bytes 405512 | tf_op jit(solution)/shard_map/ppermute | solution.py:19
  20.7 2.4 %collective-permute-start.2 = (f32[44,6,128]{2,1,0:T(8,128)S(1)}, f32[44,6,128]{2,1,0:T(8,128)S(1)}, u32[]{:S(2)}, u32[]{:S(2)}) collective-permute-start(f32[44,6,128]{2,1,0:T(8,128)S(1)} %get-tuple-element.9), channel_id=1, source_target_pairs={{0,1},{1,2},{2,3},{3,4},{4,5},{5,6},{6,7},{8,9},{9,10},{10,11},{11... | collective-permute-start | bytes 405512 | tf_op jit(solution)/shard_map/ppermute | solution.py:17
  23.1 0.1 pad_maximum_fusion.4
  23.2 3.2 %collective-permute-start.7 = (f32[42,5,256]{2,1,0:T(8,128)S(1)}, f32[42,5,256]{2,1,0:T(8,128)S(1)}, u32[]{:S(2)}, u32[]{:S(2)}) collective-permute-start(f32[42,5,256]{2,1,0:T(8,128)S(1)} %get-tuple-element.6), channel_id=1, source_target_pairs={{1,0},{2,1},{3,2},{4,3},{5,4},{6,5},{7,6},{9,8},{10,9},{11,10},{12... | collective-permute-start | bytes 645128 | tf_op jit(solution)/shard_map/ppermute | solution.py:19
  26.4 1.9 %collective-permute-start.6 = (f32[42,5,256]{2,1,0:T(8,128)S(1)}, f32[42,5,256]{2,1,0:T(8,128)S(1)}, u32[]{:S(2)}, u32[]{:S(2)}) collective-permute-start(f32[42,5,256]{2,1,0:T(8,128)S(1)} %get-tuple-element.5), channel_id=1, source_target_pairs={{0,1},{1,2},{2,3},{3,4},{4,5},{5,6},{6,7},{8,9},{9,10},{10,11},{11... | collective-permute-start | bytes 645128 | tf_op jit(solution)/shard_map/ppermute | solution.py:17
  28.3 0.1 pad_maximum_fusion.1
  28.5 2.6 %collective-permute-done.7 = f32[42,5,256]{2,1,0:T(8,128)S(1)} collective-permute-done((f32[42,5,256]{2,1,0:T(8,128)S(1)}, f32[42,5,256]{2,1,0:T(8,128)S(1)}, u32[]{:S(2)}, u32[]{:S(2)}) %collective-permute-start.7) | collective-permute-done | bytes 215072 | tf_op jit(solution)/shard_map/ppermute | solution.py:19
  31.1 3.8 %collective-permute-done.6 = f32[42,5,256]{2,1,0:T(8,128)S(1)} collective-permute-done((f32[42,5,256]{2,1,0:T(8,128)S(1)}, f32[42,5,256]{2,1,0:T(8,128)S(1)}, u32[]{:S(2)}, u32[]{:S(2)}) %collective-permute-start.6) | collective-permute-done | bytes 215072 | tf_op jit(solution)/shard_map/ppermute | solution.py:17
  34.9 0.3 pad_maximum_fusion
  35.3 0.5 fusion.1
  35.8 0.5 fusion.6
  36.3 0.5 fusion.11
  36.8 0.5 fusion.16
  37.3 0.0 copy-start
  37.4 0.0 copy-start.1
  37.4 0.5 fusion.21
  37.9 0.5 copy-done
  38.4 0.2 copy-done.1
  38.5 0.3 add_reduce_fusion
  38.9 0.0 copy-start.2
  38.9 0.9 %broadcast_in_dim.156 = f32[32,1,8192]{2,1,0:T(1,128)S(1)} broadcast(f32[8192]{0:T(1024)S(1)} %pad_maximum_fusion.5), dimensions={2} | broadcast | bytes 1081344 | tf_op jit(solution)/shard_map/broadcast_in_dim | solution.py:29
  39.8 41.0 %all_to_all.6 = f32[32,1,8192]{2,1,0:T(1,128)S(1)} all-to-all(f32[32,1,8192]{2,1,0:T(1,128)S(1)} %broadcast_in_dim.156), channel_id=1, replica_groups=mesh['py'=32,'px'=8] {'py'}, dimensions={0} | all-to-all | bytes 2097152 | tf_op jit(solution)/shard_map/all_to_all | solution.py:28
  80.9 0.7 reduce_sum.29
  81.6 0.9 %subtract_multiply_fusion = f32[32,32,128]{2,1,0:T(8,128)} fusion(f32[32,32,128]{2,1,0:T(8,128)S(1)} %get-tuple-element.4, f32[32,128]{1,0:T(8,128)S(1)} %get-tuple-element.14, f32[32,128]{1,0:T(8,128)S(1)} %get-tuple-element.13), kind=kLoop, calls=%fused_computation.56 | loop fusion | flops 262144 | bytes 1081344 | tf_op jit(solution)/shard_map/mul | solution.py:96
  (21 shorter events, 0.2 us)
Async XLA Ops:
  0.6 8.1 %copy-start.3 = (f32[32,32,128]{2,1,0:T(8,128)S(1)}, f32[32,32,128]{2,1,0:T(8,128)}, u32[]{:S(2)}) copy-start(f32[32,32,128]{2,1,0:T(8,128)} %param.3) | copy-start | bytes 1572868
  2.9 20.2 %collective-permute-start.5 = (f32[5,32,256]{2,1,0:T(8,128)S(1)}, f32[5,32,256]{2,1,0:T(8,128)S(1)}, u32[]{:S(2)}, u32[]{:S(2)}) collective-permute-start(f32[5,32,256]{2,1,0:T(8,128)S(1)} %get-tuple-element.8), channel_id=1, source_target_pairs={{8,0},{16,8},{24,16},{32,24},{40,32},{48,40},{56,48},{64,56},{72,6... | collective-permute-start | bytes 491528 | tf_op jit(solution)/shard_map/ppermute | solution.py:19
  4.2 18.9 %collective-permute-start.4 = (f32[5,32,256]{2,1,0:T(8,128)S(1)}, f32[5,32,256]{2,1,0:T(8,128)S(1)}, u32[]{:S(2)}, u32[]{:S(2)}) collective-permute-start(f32[5,32,256]{2,1,0:T(8,128)S(1)} %get-tuple-element.7), channel_id=1, source_target_pairs={{0,8},{8,16},{16,24},{24,32},{32,40},{40,48},{48,56},{56,64},{64,7... | collective-permute-start | bytes 491528 | tf_op jit(solution)/shard_map/ppermute | solution.py:17
  8.8 5.6 %collective-permute-start = (f32[6,32,128]{2,1,0:T(8,128)S(1)}, f32[6,32,128]{2,1,0:T(8,128)S(1)}, u32[]{:S(2)}, u32[]{:S(2)}) collective-permute-start(f32[6,32,128]{2,1,0:T(8,128)S(1)} %get-tuple-element.12), channel_id=1, source_target_pairs={{0,8},{8,16},{16,24},{24,32},{32,40},{40,48},{48,56},{56,64},{64,7... | collective-permute-start | bytes 294920 | tf_op jit(solution)/shard_map/ppermute | solution.py:17
  12.2 6.5 %collective-permute-start.1 = (f32[6,32,128]{2,1,0:T(8,128)S(1)}, f32[6,32,128]{2,1,0:T(8,128)S(1)}, u32[]{:S(2)}, u32[]{:S(2)}) collective-permute-start(f32[6,32,128]{2,1,0:T(8,128)S(1)} %get-tuple-element.11), channel_id=1, source_target_pairs={{8,0},{16,8},{24,16},{32,24},{40,32},{48,40},{56,48},{64,56},{72,6... | collective-permute-start | bytes 294920 | tf_op jit(solution)/shard_map/ppermute | solution.py:19
  18.8 9.5 %collective-permute-start.3 = (f32[44,6,128]{2,1,0:T(8,128)S(1)}, f32[44,6,128]{2,1,0:T(8,128)S(1)}, u32[]{:S(2)}, u32[]{:S(2)}) collective-permute-start(f32[44,6,128]{2,1,0:T(8,128)S(1)} %get-tuple-element.10), channel_id=1, source_target_pairs={{1,0},{2,1},{3,2},{4,3},{5,4},{6,5},{7,6},{9,8},{10,9},{11,10},{12... | collective-permute-start | bytes 405512 | tf_op jit(solution)/shard_map/ppermute | solution.py:19
  20.7 7.6 %collective-permute-start.2 = (f32[44,6,128]{2,1,0:T(8,128)S(1)}, f32[44,6,128]{2,1,0:T(8,128)S(1)}, u32[]{:S(2)}, u32[]{:S(2)}) collective-permute-start(f32[44,6,128]{2,1,0:T(8,128)S(1)} %get-tuple-element.9), channel_id=1, source_target_pairs={{0,1},{1,2},{2,3},{3,4},{4,5},{5,6},{6,7},{8,9},{9,10},{10,11},{11... | collective-permute-start | bytes 405512 | tf_op jit(solution)/shard_map/ppermute | solution.py:17
  23.2 7.9 %collective-permute-start.7 = (f32[42,5,256]{2,1,0:T(8,128)S(1)}, f32[42,5,256]{2,1,0:T(8,128)S(1)}, u32[]{:S(2)}, u32[]{:S(2)}) collective-permute-start(f32[42,5,256]{2,1,0:T(8,128)S(1)} %get-tuple-element.6), channel_id=1, source_target_pairs={{1,0},{2,1},{3,2},{4,3},{5,4},{6,5},{7,6},{9,8},{10,9},{11,10},{12... | collective-permute-start | bytes 645128 | tf_op jit(solution)/shard_map/ppermute | solution.py:19
  26.4 8.6 %collective-permute-start.6 = (f32[42,5,256]{2,1,0:T(8,128)S(1)}, f32[42,5,256]{2,1,0:T(8,128)S(1)}, u32[]{:S(2)}, u32[]{:S(2)}) collective-permute-start(f32[42,5,256]{2,1,0:T(8,128)S(1)} %get-tuple-element.5), channel_id=1, source_target_pairs={{0,1},{1,2},{2,3},{3,4},{4,5},{5,6},{6,7},{8,9},{9,10},{10,11},{11... | collective-permute-start | bytes 645128 | tf_op jit(solution)/shard_map/ppermute | solution.py:17
  37.3 1.0 %copy-start = (f32[32,32,128]{2,1,0:T(8,128)S(1)}, f32[32,32,128]{2,1,0:T(8,128)}, u32[]{:S(2)}) copy-start(f32[32,32,128]{2,1,0:T(8,128)} %param.5) | copy-start | bytes 1572868
  37.4 1.2 %copy-start.1 = (f32[32,32,128]{2,1,0:T(8,128)S(1)}, f32[32,32,128]{2,1,0:T(8,128)}, u32[]{:S(2)}) copy-start(f32[32,32,128]{2,1,0:T(8,128)} %param.4) | copy-start | bytes 1572868
  38.9 42.7 %copy-start.2 = (f32[32,32,128]{2,1,0:T(8,128)}, f32[32,32,128]{2,1,0:T(8,128)S(1)}, u32[]{:S(2)}) copy-start(f32[32,32,128]{2,1,0:T(8,128)S(1)} %get-tuple-element.4) | copy-start | bytes 1572868
where the time goes:
time: 83.2 us; the launch traced here: 82.5 us
  blocking collectives  41 us (49%)
  starting transfers between devices  19.9 us (24%)
  waiting for transfers between devices  11.5 us (14%)
  other arithmetic  5.04 us (6%)
  local copies, waits for them, and re-layouts  3.99 us (5%)
  between operations  0.94 us (1%)
    all_to_all x1, blocking collectives, sent_to_all(): lax.all_to_all(jnp.broadcast_to(shard[None], (length, *shard.shape)), axi...  41 us
    ppermute x4, starting transfers between devices, with_halo(): lax.ppermute(tail, axis, [(i, (i + 1) % count) for i in range(ends)])  12.3 us
    ppermute x4, starting transfers between devices, with_halo(): lax.ppermute(head, axis, [((i + 1) % count, i) for i in range(ends)])  7.66 us
    ppermute x4, waiting for transfers between devices, with_halo(): lax.ppermute(head, axis, [((i + 1) % count, i) for i in range(ends)])  6.92 us
    ppermute x4, waiting for transfers between devices, with_halo(): lax.ppermute(tail, axis, [(i, (i + 1) % count) for i in range(ends)])  4.63 us
    select_n x5, other arithmetic, per_device(): values = jnp.where(keep_cells.reshape((-1,) + (1,) * 1), values, 0.0)  2.55 us
    unnamed x11, local copies, waits for them, and re-layouts  1.9 us
  transfers between devices with their start and end apart: 8, of which 4 were waited for; matrix products, arithmetic and copies ran while one was open for 0% of the time, Pallas kernels for 0%

commit v1 on v0

v1 whole, which is shorter than its diff:
```python
import functools

import jax
import jax.numpy as jnp
from jax import lax
from jax.experimental import pallas as pl
from jax.experimental.pallas import tpu as pltpu
from jax.sharding import PartitionSpec as P

STEPS = 6
EPS = 1e-4
XS = 4
ROWS, COLS, LEV = 32, 32, 128
TOP, LEFT = STEPS, 8
HIGH, WIDE = ROWS + 2 * STEPS, COLS + 2 * LEFT
MESH = pl.DeviceIdType.MESH
SIDES = [(a, b) for a in (-1, 0, 1) for b in (-1, 0, 1) if a or b]


def span(side, own, first, deep):
    if side == 0:
        return first, first, own
    if side > 0:
        return first + own - deep, first - deep, deep
    return first, first + own, deep


def piece(a, b, deep):
    deep_rows = deep_cols = deep
    if a and b:
        deep_rows = deep_cols = deep - 1
    rs, rd, rn = span(a, ROWS, TOP, deep_rows)
    cs, cd, cn = span(b, COLS, LEFT, deep_cols)
    return (pl.ds(rs, rn), pl.ds(cs, cn)), (pl.ds(rd, rn), pl.ds(cd, cn))


def merged(means, spreads, each):
    count = len(means)
    mean = sum(means[1:], means[0]) * (1.0 / count)
    spread = sum(spreads[1:], spreads[0])
    for m in means:
        spread = spread + each * (m - mean) * (m - mean)
    return mean, spread


def kernel(npy, npx, d_hbm, c_hbm, s_hbm, a_out, e_out, dt, cs, part, xin, zmine, zin,
           load_sem, hs_sem, hr_sem, xs_sem, xr_sem, zs_sem, zr_sem):
    py, px = lax.axis_index("py"), lax.axis_index("px")
    zs = npy // XS
    z, x = py // XS, lax.rem(py, XS)
    own = (pl.ds(TOP, ROWS), pl.ds(LEFT, COLS))
    loads = [
        pltpu.make_async_copy(d_hbm, dt.at[(0, *own)], load_sem.at[0]),
        pltpu.make_async_copy(c_hbm, cs.at[(0, *own)], load_sem.at[1]),
        pltpu.make_async_copy(s_hbm, cs.at[(1, *own)], load_sem.at[2]),
    ]
    for load in loads:
        load.start()

    def there(a, b):
        ok = None
        for side, at, count in ((a, py, npy), (b, px, npx)):
            if side:
                good = (at < count - 1) if side > 0 else (at > 0)
                ok = good if ok is None else ok & good
        return ok

    def xpeer(k):
        return {"py": z * XS + lax.rem(x + k, XS), "px": px}

    def zpeer(k):
        return {"py": lax.rem(z + k, zs) * XS + x, "px": px}

    barrier = pltpu.get_barrier_semaphore()
    for a, b in SIDES:
        @pl.when(there(a, b))
        def _():
            pl.semaphore_signal(barrier, inc=1, device_id={"py": py + a, "px": px + b}, device_id_type=MESH)
    for k in range(1, XS):
        pl.semaphore_signal(barrier, inc=1, device_id=xpeer(k), device_id_type=MESH)
    for k in range(1, zs):
        pl.semaphore_signal(barrier, inc=1, device_id=zpeer(k), device_id_type=MESH)

    for a in (-1, 1):
        @pl.when(jnp.logical_not(there(a, 0)))
        def _():
            rows = pl.ds(0, TOP) if a < 0 else pl.ds(TOP + ROWS, STEPS)
            dt[0, rows] = jnp.zeros((STEPS, WIDE, LEV), jnp.float32)
            cs[:, rows] = jnp.zeros((2, STEPS, WIDE, LEV), jnp.float32)
    for b in (-1, 1):
        @pl.when(jnp.logical_not(there(0, b)))
        def _():
            cols = pl.ds(0, LEFT) if b < 0 else pl.ds(LEFT + COLS, LEFT)
            dt[0, :, cols] = jnp.zeros((HIGH, LEFT, LEV), jnp.float32)
            cs[:, :, cols] = jnp.zeros((2, HIGH, LEFT, LEV), jnp.float32)

    for load in loads:
        load.wait()
    near = (py > 0).astype(jnp.int32) + (py < npy - 1).astype(jnp.int32)
    beside = (px > 0).astype(jnp.int32) + (px < npx - 1).astype(jnp.int32)
    pl.semaphore_wait(barrier, (near + 1) * (beside + 1) - 1 + XS - 1 + zs - 1)

    def halo(a, b):
        at = SIDES.index((a, b))
        (fr, fc), (tr, tc) = piece(a, b, STEPS)
        (gr, gc), (ur, uc) = piece(a, b, STEPS - 1)
        to = {"py": py + a, "px": px + b}
        return [
            pltpu.make_async_remote_copy(dt.at[0, fr, fc], dt.at[0, tr, tc], hs_sem.at[2 * at], hr_sem.at[2 * at], device_id=to, device_id_type=MESH),
            pltpu.make_async_remote_copy(cs.at[:, gr, gc], cs.at[:, ur, uc], hs_sem.at[2 * at + 1], hr_sem.at[2 * at + 1], device_id=to, device_id_type=MESH),
        ]

    order = [(a, b) for a, b in SIDES if a and b] + [(0, 1), (0, -1), (1, 0), (-1, 0)]
    for a, b in order:
        @pl.when(there(a, b))
        def _():
            for copy in halo(a, b):
                copy.start()

    def arrive(a, b):
        @pl.when(there(a, b))
        def _():
            for copy in halo(-a, -b):
                copy.wait_recv()

    def rows_of(step, low, count):
        @pl.loop(0, count)
        def _(i):
            r = low + i
            mid = dt[step, r]
            spread = dt[step, r - 1] + dt[step, r + 1] + (pltpu.roll(mid, 1, 0) + pltpu.roll(mid, WIDE - 1, 0)) - 4.0 * mid
            dt[step + 1, r] = mid + cs[0, r] * spread + cs[1, r]

    arrive(0, -1)
    arrive(0, 1)
    for step in range(STEPS):
        rows_of(step, TOP + step + 1, ROWS - 2 * (step + 1))
    block = pl.ds(LEFT, COLS)
    inner = ROWS - 2 * STEPS
    guess = lax.fori_loop(0, inner, lambda i, v: v + dt[STEPS, 2 * STEPS + i, block], jnp.zeros((COLS, LEV), jnp.float32)) * (1.0 / inner)

    def gather(low, count, totals):
        def add(i, totals):
            moved = dt[STEPS, low + i, block] - guess
            return totals[0] + moved, totals[1] + moved * moved
        return lax.fori_loop(0, count, add, totals)

    zero = jnp.zeros((COLS, LEV), jnp.float32)
    totals = gather(2 * STEPS, inner, (zero, zero))
    for a in (-1, 1):
        for b in (-1, 0, 1):
            arrive(a, b)
        for step in range(STEPS):
            low = step + 1 if a < 0 else TOP + ROWS - step - 1
            rows_of(step, low, STEPS)
        totals = gather(TOP if a < 0 else TOP + ROWS - STEPS, STEPS, totals)
    offset = totals[0] * (1.0 / ROWS)
    mean, spread = guess + offset, totals[1] - totals[0] * offset
    part[0] = mean
    part[1] = spread

    def over(peer, count, mine, got, send, recv, each):
        copies = []
        for k in range(1, count):
            copies.append(pltpu.make_async_remote_copy(mine, got.at[k - 1], send.at[k - 1], recv.at[k - 1], device_id=peer(k), device_id_type=MESH))
        for copy in copies:
            copy.start()
        for copy in copies:
            copy.wait_recv()
        means, spreads = [mine[0]] + [got[k, 0] for k in range(count - 1)], [mine[1]] + [got[k, 1] for k in range(count - 1)]
        return copies, *merged(means, spreads, each)

    sent, mean, spread = over(xpeer, XS, part, xin, xs_sem, xr_sem, float(ROWS))
    zmine[0] = mean
    zmine[1] = spread
    sent_z, mean, spread = over(zpeer, zs, zmine, zin, zs_sem, zr_sem, float(ROWS * XS))
    scale = lax.rsqrt(spread * (1.0 / (ROWS * npy)) + EPS)

    @pl.loop(0, ROWS)
    def _(i):
        value = dt[STEPS, TOP + i, block]
        e_out[i] = value
        a_out[i] = (value - mean) * scale

    for copy in sent + sent_z:
        copy.wait_send()
    for a, b in order:
        @pl.when(there(a, b))
        def _():
            for copy in halo(a, b):
                copy.wait_send()


def solution(mesh):
    npy, npx = mesh.shape["py"], mesh.shape["px"]
    zs = npy // XS

    def per_device(density, conductance, source):
        shape = jax.ShapeDtypeStruct((ROWS, COLS, LEV), jnp.float32)
        f32 = jnp.float32
        dma = pltpu.SemaphoreType.DMA
        return pl.pallas_call(
            functools.partial(kernel, npy, npx),
            name="diffuse",
            out_shape=(shape, shape),
            in_specs=[pl.BlockSpec(memory_space=pl.ANY)] * 3,
            out_specs=[pl.BlockSpec(memory_space=pltpu.VMEM)] * 2,
            scratch_shapes=[
                pltpu.VMEM((STEPS + 1, HIGH, WIDE, LEV), f32),
                pltpu.VMEM((2, HIGH, WIDE, LEV), f32),
                pltpu.VMEM((2, COLS, LEV), f32),
                pltpu.VMEM((XS - 1, 2, COLS, LEV), f32),
                pltpu.VMEM((2, COLS, LEV), f32),
                pltpu.VMEM((zs - 1, 2, COLS, LEV), f32),
                dma((3,)), dma((16,)), dma((16,)),
                dma((XS - 1,)), dma((XS - 1,)), dma((zs - 1,)), dma((zs - 1,)),
            ],
            compiler_params=pltpu.CompilerParams(collective_id=0, has_side_effects=True),
        )(density, conductance, source)

    spec = P("py", "px", None)
    return jax.shard_map(per_device, mesh=mesh, in_specs=(spec,) * 3, out_specs=(spec, spec), check_vma=False)
```

time: 83.2 us -> 36.3 us (0.44)
  blocking collectives: 41 us -> 0 us
  Pallas kernels: 0 us -> 32.8 us
  starting transfers between devices: 19.9 us -> 0 us
  waiting for transfers between devices: 11.5 us -> 0 us
  other arithmetic: 5.04 us -> 0 us
  local copies, waits for them, and re-layouts: 3.99 us -> 2.72 us
    all_to_all x1 -> x0, blocking collectives: 41 us -> none  [sent_to_all(): lax.all_to_all(jnp.broadcast_to(shard[None], (length, *shard.shape)), axi...]
    pallas_call x0 -> x1, Pallas kernels: none -> 32.8 us  [per_device(): pl.pallas_call(functools.partial(kernel, npy, npx), name='diffuse', out_s...]
    ppermute x8 -> x0, starting transfers between devices: 19.9 us -> none  [the longest x4 12.3 us: with_halo(): lax.ppermute(tail, axis, [(i, (i + 1) % count) for i in range(ends)])]
    ppermute x8 -> x0, waiting for transfers between devices: 11.5 us -> none  [the longest x4 6.92 us: with_halo(): lax.ppermute(head, axis, [((i + 1) % count, i) for i in range(ends)])]
    select_n x5 -> x0, other arithmetic: 2.55 us -> none  [per_device(): values = jnp.where(keep_cells.reshape((-1,) + (1,) * 1), values, 0.0)]
    concatenate x2 -> x0, local copies, waits for them, and re-layouts: 1.09 us -> none  [the longest x1 1.08 us: per_device(): jnp.concatenate([conductance, source], axis=2)]
    reduce_sum x2 -> x0, other arithmetic: 1.03 us -> none  [the longest x1 0.7 us: over_copies(): return sent_to_all(shard, axis).sum(axis=0)]
    broadcast_in_dim x1 -> x0, local copies, waits for them, and re-layouts: 0.93 us -> none  [sent_to_all(): jnp.broadcast_to(shard[None], (length, *shard.shape))]
  transfers between devices with their start and end apart: 8 -> 0, of which waited for: 4 -> 0; matrix products, arithmetic and copies ran while one was open for 0% -> 0% of each run, Pallas kernels for 0% -> 0%
where the time goes in v1:
time: 36.3 us; the launch traced here: 36.1 us
  Pallas kernels  32.8 us (90%)
  local copies, waits for them, and re-layouts  2.72 us (7%)
  between operations  0.65 us (2%)
    pallas_call x1, Pallas kernels, per_device(): pl.pallas_call(functools.partial(kernel, npy, npx), name='diffuse', out_s...  32.8 us
    unnamed x4, local copies, waits for them, and re-layouts  2.72 us

profile of v1, /device:TPU:8, one launch (start us, length us, event | category | flops | bytes accessed | tf_op | source)
XLA Modules:
  0.0 36.1 jit_solution(9684375972306180285)
XLA Ops:
  0.6 32.8 %diffuse.1 = (f32[32,32,128]{2,1,0:T(8,128)}, f32[32,32,128]{2,1,0:T(8,128)}) custom-call(f32[32,32,128]{2,1,0:T(8,128)} %d_hbm.1, f32[32,32,128]{2,1,0:T(8,128)} %c_hbm.1, f32[32,32,128]{2,1,0:T(8,128)} %s_hbm.1), custom_call_target="tpu_custom_call" | custom-call | tf_op jit(solution)/shard_map/diffuse/pallas_call | solution.py:202
  33.4 0.0 copy-start
  33.4 1.9 %copy.7 = f32[32,32,128]{2,1,0:T(8,128)} copy(f32[32,32,128]{2,1,0:T(8,128)} %get-tuple-element.4) | data formatting | bytes 1048576
  35.3 0.0 copy-done
  35.3 0.8 %copy.8 = f32[32,32,128]{2,1,0:T(8,128)} copy(f32[32,32,128]{2,1,0:T(8,128)S(1)} %copy-done) | data formatting | bytes 1048576
Async XLA Ops:
  33.4 1.9 %copy-start = (f32[32,32,128]{2,1,0:T(8,128)S(1)}, f32[32,32,128]{2,1,0:T(8,128)}, u32[]{:S(2)}) copy-start(f32[32,32,128]{2,1,0:T(8,128)} %get-tuple-element.5) | copy-start | bytes 1572868

commit v2 on v1

--- a/solution.py
+++ b/solution.py
@@ -43,7 +43,7 @@
     return mean, spread
 
 
-def kernel(npy, npx, d_hbm, c_hbm, s_hbm, a_out, e_out, dt, cs, part, xin, zmine, zin,
+def kernel(npy, npx, d_hbm, c_hbm, s_hbm, e_out, stats, dt, cs, part, xin, zmine, zin,
            load_sem, hs_sem, hr_sem, xs_sem, xr_sem, zs_sem, zr_sem):
     py, px = lax.axis_index("py"), lax.axis_index("px")
     zs = npy // XS
@@ -94,11 +94,13 @@
             dt[0, :, cols] = jnp.zeros((HIGH, LEFT, LEV), jnp.float32)
             cs[:, :, cols] = jnp.zeros((2, HIGH, LEFT, LEV), jnp.float32)
 
-    for load in loads:
-        load.wait()
+    with jax.named_scope("loads"):
+        for load in loads:
+            load.wait()
     near = (py > 0).astype(jnp.int32) + (py < npy - 1).astype(jnp.int32)
     beside = (px > 0).astype(jnp.int32) + (px < npx - 1).astype(jnp.int32)
-    pl.semaphore_wait(barrier, (near + 1) * (beside + 1) - 1 + XS - 1 + zs - 1)
+    with jax.named_scope("barrier"):
+        pl.semaphore_wait(barrier, (near + 1) * (beside + 1) - 1 + XS - 1 + zs - 1)
 
     def halo(a, b):
         at = SIDES.index((a, b))
@@ -111,11 +113,12 @@
         ]
 
     order = [(a, b) for a, b in SIDES if a and b] + [(0, 1), (0, -1), (1, 0), (-1, 0)]
-    for a, b in order:
-        @pl.when(there(a, b))
-        def _():
-            for copy in halo(a, b):
-                copy.start()
+    with jax.named_scope("sends"):
+        for a, b in order:
+            @pl.when(there(a, b))
+            def _():
+                for copy in halo(a, b):
+                    copy.start()
 
     def arrive(a, b):
         @pl.when(there(a, b))
@@ -131,10 +134,12 @@
             spread = dt[step, r - 1] + dt[step, r + 1] + (pltpu.roll(mid, 1, 0) + pltpu.roll(mid, WIDE - 1, 0)) - 4.0 * mid
             dt[step + 1, r] = mid + cs[0, r] * spread + cs[1, r]
 
-    arrive(0, -1)
-    arrive(0, 1)
-    for step in range(STEPS):
-        rows_of(step, TOP + step + 1, ROWS - 2 * (step + 1))
+    with jax.named_scope("arrive_px"):
+        arrive(0, -1)
+        arrive(0, 1)
+    with jax.named_scope("inner"):
+        for step in range(STEPS):
+            rows_of(step, TOP + step + 1, ROWS - 2 * (step + 1))
     block = pl.ds(LEFT, COLS)
     inner = ROWS - 2 * STEPS
     guess = lax.fori_loop(0, inner, lambda i, v: v + dt[STEPS, 2 * STEPS + i, block], jnp.zeros((COLS, LEV), jnp.float32)) * (1.0 / inner)
@@ -148,40 +153,47 @@
     zero = jnp.zeros((COLS, LEV), jnp.float32)
     totals = gather(2 * STEPS, inner, (zero, zero))
     for a in (-1, 1):
-        for b in (-1, 0, 1):
-            arrive(a, b)
-        for step in range(STEPS):
-            low = step + 1 if a < 0 else TOP + ROWS - step - 1
-            rows_of(step, low, STEPS)
+        with jax.named_scope("arrive_py"):
+            for b in (-1, 0, 1):
+                arrive(a, b)
+        with jax.named_scope("outer"):
+            for step in range(STEPS):
+                low = step + 1 if a < 0 else TOP + ROWS - step - 1
+                rows_of(step, low, STEPS)
         totals = gather(TOP if a < 0 else TOP + ROWS - STEPS, STEPS, totals)
     offset = totals[0] * (1.0 / ROWS)
     mean, spread = guess + offset, totals[1] - totals[0] * offset
     part[0] = mean
     part[1] = spread
 
-    def over(peer, count, mine, got, send, recv, each):
+    def over(peer, count, mine, got, send, recv, each, meanwhile=None):
         copies = []
         for k in range(1, count):
             copies.append(pltpu.make_async_remote_copy(mine, got.at[k - 1], send.at[k - 1], recv.at[k - 1], device_id=peer(k), device_id_type=MESH))
         for copy in copies:
             copy.start()
+        if meanwhile:
+            meanwhile()
         for copy in copies:
             copy.wait_recv()
         means, spreads = [mine[0]] + [got[k, 0] for k in range(count - 1)], [mine[1]] + [got[k, 1] for k in range(count - 1)]
         return copies, *merged(means, spreads, each)
 
-    sent, mean, spread = over(xpeer, XS, part, xin, xs_sem, xr_sem, float(ROWS))
+    def put_end():
+        @pl.loop(0, ROWS)
+        def _(i):
+            e_out[i] = dt[STEPS, TOP + i, block]
+
+    with jax.named_scope("over_x"):
+        sent, mean, spread = over(xpeer, XS, part, xin, xs_sem, xr_sem, float(ROWS), put_end)
     zmine[0] = mean
     zmine[1] = spread
-    sent_z, mean, spread = over(zpeer, zs, zmine, zin, zs_sem, zr_sem, float(ROWS * XS))
+    with jax.named_scope("over_z"):
+        sent_z, mean, spread = over(zpeer, zs, zmine, zin, zs_sem, zr_sem, float(ROWS * XS))
     scale = lax.rsqrt(spread * (1.0 / (ROWS * npy)) + EPS)
 
-    @pl.loop(0, ROWS)
-    def _(i):
-        value = dt[STEPS, TOP + i, block]
-        e_out[i] = value
-        a_out[i] = (value - mean) * scale
-
+    stats[0] = mean
+    stats[1] = scale
     for copy in sent + sent_z:
         copy.wait_send()
     for a, b in order:
@@ -191,6 +203,21 @@
                 copy.wait_send()
 
 
+def finish(end, stats, a_out, e_out, held, sem):
+    whole = pltpu.make_async_copy(end, e_out, sem.at[0])
+    whole.start()
+    mean, scale = stats[0], stats[1]
+
+    @pl.loop(0, ROWS)
+    def _(i):
+        held[i] = (end[i] - mean) * scale
+
+    lines = pltpu.make_async_copy(held, a_out, sem.at[1])
+    lines.start()
+    whole.wait()
+    lines.wait()
+
+
 def solution(mesh):
     npy, npx = mesh.shape["py"], mesh.shape["px"]
     zs = npy // XS
@@ -199,10 +226,10 @@
         shape = jax.ShapeDtypeStruct((ROWS, COLS, LEV), jnp.float32)
         f32 = jnp.float32
         dma = pltpu.SemaphoreType.DMA
-        return pl.pallas_call(
+        end, stats = pl.pallas_call(
             functools.partial(kernel, npy, npx),
             name="diffuse",
-            out_shape=(shape, shape),
+            out_shape=(pltpu.VMEM((ROWS, COLS, LEV), f32), pltpu.VMEM((2, COLS, LEV), f32)),
             in_specs=[pl.BlockSpec(memory_space=pl.ANY)] * 3,
             out_specs=[pl.BlockSpec(memory_space=pltpu.VMEM)] * 2,
             scratch_shapes=[
@@ -217,6 +244,14 @@
             ],
             compiler_params=pltpu.CompilerParams(collective_id=0, has_side_effects=True),
         )(density, conductance, source)
+        return pl.pallas_call(
+            finish,
+            name="finish",
+            out_shape=(shape, shape),
+            in_specs=[pl.BlockSpec(memory_space=pltpu.VMEM)] * 2,
+            out_specs=[pl.BlockSpec(memory_space=pl.ANY)] * 2,
+            scratch_shapes=[pltpu.VMEM((ROWS, COLS, LEV), f32), dma((2,))],
+        )(*(pltpu.with_memory_space_constraint(v, pltpu.VMEM) for v in (end, stats)))
 
     spec = P("py", "px", None)
     return jax.shard_map(per_device, mesh=mesh, in_specs=(spec,) * 3, out_specs=(spec, spec), check_vma=False)

time: 36.3 us -> 33.4 us (0.920)
  local copies, waits for them, and re-layouts: 2.72 us -> 0 us
    unnamed x4 -> x0, local copies, waits for them, and re-layouts: 2.72 us -> none
    pallas_call x1, Pallas kernels: 32.8 us -> 31.6 us  [per_device(): pl.pallas_call(functools.partial(kernel, npy, npx), name='diffuse', out_s...]
    pallas_call x0 -> x1, Pallas kernels: none -> 1.01 us  [per_device(): pl.pallas_call(finish, name='finish', out_shape=(shape, shape), in_specs=...]
where the time goes in v2:
time: 33.4 us; the launch traced here: 33.2 us
  Pallas kernels  32.6 us (98%)
  between operations  0.64 us (2%)
    pallas_call x1, Pallas kernels, per_device(): pl.pallas_call(functools.partial(kernel, npy, npx), name='diffuse', out_s...  31.6 us
    pallas_call x1, Pallas kernels, per_device(): pl.pallas_call(finish, name='finish', out_shape=(shape, shape), in_specs=...  1.01 us

profile of v2, /device:TPU:8, one launch (start us, length us, event | category | flops | bytes accessed | tf_op | source)
XLA Modules:
  0.0 33.2 jit_solution(14577672441985970176)
XLA Ops:
  0.6 31.6 %diffuse.1 = (f32[32,32,128]{2,1,0:T(8,128)S(1)}, f32[2,32,128]{2,1,0:T(8,128)S(1)}) custom-call(f32[32,32,128]{2,1,0:T(8,128)} %d_hbm.1, f32[32,32,128]{2,1,0:T(8,128)} %c_hbm.1, f32[32,32,128]{2,1,0:T(8,128)} %s_hbm.1), custom_call_target="tpu_custom_call" | custom-call | tf_op jit(solution)/shard_map/diffuse/pallas_call | solution.py:229
  32.2 1.0 %finish.1 = (f32[32,32,128]{2,1,0:T(8,128)}, f32[32,32,128]{2,1,0:T(8,128)}) custom-call(f32[32,32,128]{2,1,0:T(8,128)S(1)} %get-tuple-element.4.end, f32[2,32,128]{2,1,0:T(8,128)S(1)} %get-tuple-element.5.stats), custom_call_target="tpu_custom_call" | custom-call | tf_op jit(solution)/shard_map/finish/pallas_call | solution.py:247

commit v3 on v2

v3 whole, which is shorter than its diff:
```python
import functools

import jax
import jax.numpy as jnp
from jax import lax
from jax.experimental import pallas as pl
from jax.experimental.pallas import tpu as pltpu
from jax.sharding import PartitionSpec as P

STEPS = 6
EPS = 1e-4
XS = 4
ROWS, COLS, LEV = 32, 32, 128
TOP, LEFT = STEPS, 8
HIGH, WIDE = ROWS + 2 * STEPS, COLS + 2 * LEFT
HALF = COLS // 2
MESH = pl.DeviceIdType.MESH
SIDES = [(a, b) for a in (-1, 0, 1) for b in (-1, 0, 1) if a or b]
GROUPS = (((1, 3), (1, 2)), ((4, 5), (3, 4)), ((6, 6), (5, 5)))
DIAGONALS = ((1, 2, 3), (4, 5), (6,))
CORNER_D = ((1, 2, 5), (3, 5, 3))
CORNER_CS = ((1, 2, 4), (3, 4, 2))


def reach(side, size, start, first, last):
    length = last - first + 1
    if side > 0:
        return pl.ds(start + size - last, length), pl.ds(start - last, length)
    return pl.ds(start + first - 1, length), pl.ds(start + size + first - 1, length)


def halo_pieces(a, b):
    rows, cols = pl.ds(TOP, ROWS), pl.ds(LEFT, COLS)
    out = []
    if a and b:
        for which, pieces in ((0, CORNER_D), (1, CORNER_CS)):
            for first, last, wide in pieces:
                (fr, tr), (fc, tc) = reach(a, ROWS, TOP, first, last), reach(b, COLS, LEFT, 1, wide)
                out.append((which, (fr, fc), (tr, tc)))
    elif b:
        for which, deep in ((0, STEPS), (1, STEPS - 1)):
            fc, tc = reach(b, COLS, LEFT, 1, deep)
            out.append((which, (rows, fc), (rows, tc)))
    else:
        for group in GROUPS:
            for which, (first, last) in enumerate(group):
                fr, tr = reach(a, ROWS, TOP, first, last)
                out.append((which, (fr, cols), (tr, cols)))
    return out


PIECES = {side: halo_pieces(*side) for side in SIDES}
FIRST = {}
for _side in SIDES:
    FIRST[_side] = sum(len(PIECES[s]) for s in FIRST)
COPIES = sum(len(p) for p in PIECES.values())


def merged(means, spreads, each):
    mean = sum(means[1:], means[0]) * (1.0 / len(means))
    spread = sum(spreads[1:], spreads[0])
    for m in means:
        spread = spread + each * (m - mean) * (m - mean)
    return mean, spread


def kernel(npy, npx, d_hbm, c_hbm, s_hbm, e_out, stats, dt, cs, part, mid_part, xin, zin,
           load_sem, hs_sem, hr_sem, xs_sem, xr_sem, zs_sem, zr_sem):
    py, px = lax.axis_index("py"), lax.axis_index("px")
    zs = npy // XS
    z, x = py // XS, lax.rem(py, XS)
    own = (pl.ds(TOP, ROWS), pl.ds(LEFT, COLS))
    loads = [
        pltpu.make_async_copy(d_hbm, dt.at[(0, *own)], load_sem.at[0]),
        pltpu.make_async_copy(c_hbm, cs.at[(0, *own)], load_sem.at[1]),
        pltpu.make_async_copy(s_hbm, cs.at[(1, *own)], load_sem.at[2]),
    ]
    for load in loads:
        load.start()

    def there(a, b):
        ok = None
        for side, at, count in ((a, py, npy), (b, px, npx)):
            if side:
                good = (at < count - 1) if side > 0 else (at > 0)
                ok = good if ok is None else ok & good
        return ok

    def xpeer(k):
        return {"py": z * XS + lax.rem(x + k, XS), "px": px}

    def zpeer(k):
        return {"py": lax.rem(z + k, zs) * XS + x, "px": px}

    barrier = pltpu.get_barrier_semaphore()
    for a, b in SIDES:
        @pl.when(there(a, b))
        def _():
            pl.semaphore_signal(barrier, inc=1, device_id={"py": py + a, "px": px + b}, device_id_type=MESH)
    for k in range(1, XS):
        pl.semaphore_signal(barrier, inc=1, device_id=xpeer(k), device_id_type=MESH)
    for k in range(1, zs):
        pl.semaphore_signal(barrier, inc=1, device_id=zpeer(k), device_id_type=MESH)

    for a in (-1, 1):
        @pl.when(jnp.logical_not(there(a, 0)))
        def _():
            rows = pl.ds(0, TOP) if a < 0 else pl.ds(TOP + ROWS, STEPS)
            dt[0, rows] = jnp.zeros((STEPS, WIDE, LEV), jnp.float32)
            cs[:, rows] = jnp.zeros((2, STEPS, WIDE, LEV), jnp.float32)
    for b in (-1, 1):
        @pl.when(jnp.logical_not(there(0, b)))
        def _():
            cols = pl.ds(0, LEFT) if b < 0 else pl.ds(LEFT + COLS, LEFT)
            dt[0, :, cols] = jnp.zeros((HIGH, LEFT, LEV), jnp.float32)
            cs[:, :, cols] = jnp.zeros((2, HIGH, LEFT, LEV), jnp.float32)

    with jax.named_scope("loads"):
        for load in loads:
            load.wait()
    near = (py > 0).astype(jnp.int32) + (py < npy - 1).astype(jnp.int32)
    beside = (px > 0).astype(jnp.int32) + (px < npx - 1).astype(jnp.int32)
    with jax.named_scope("barrier"):
        pl.semaphore_wait(barrier, (near + 1) * (beside + 1) - 1 + XS - 1 + zs - 1)

    def halo(a, b, part=slice(None)):
        to = {"py": py + a, "px": px + b}
        copies = []
        for at, (which, source, target) in list(enumerate(PIECES[a, b], FIRST[a, b]))[part]:
            if which:
                src, dst = cs.at[(slice(None), *source)], cs.at[(slice(None), *target)]
            else:
                src, dst = dt.at[(0, *source)], dt.at[(0, *target)]
            copies.append(pltpu.make_async_remote_copy(src, dst, hs_sem.at[at], hr_sem.at[at], device_id=to, device_id_type=MESH))
        return copies

    order = [(0, 1), (0, -1)] + [(a, b) for a, b in SIDES if a and b] + [(1, 0), (-1, 0)]
    with jax.named_scope("sends"):
        for a, b in order:
            @pl.when(there(a, b))
            def _():
                for copy in halo(a, b):
                    copy.start()

    def arrive(a, b, part=slice(None)):
        @pl.when(there(a, b))
        def _():
            for copy in halo(-a, -b, part):
                copy.wait_recv()

    def later(above, mid, below, r):
        spread = (above + below) + (pltpu.roll(mid, 1, 0) + pltpu.roll(mid, WIDE - 1, 0)) - 4.0 * mid
        return mid + cs[0, r] * spread + cs[1, r]

    with jax.named_scope("arrive_px"):
        arrive(0, -1)
        arrive(0, 1)
    with jax.named_scope("inner"):
        for step in range(STEPS):
            low, count = TOP + step + 1, ROWS - 2 * (step + 1)

            @pl.loop(0, count // 2)
            def _(i):
                r = low + 2 * i
                lines = [dt[step, r + n] for n in range(-1, 3)]
                dt[step + 1, r] = later(*lines[:3], r)
                dt[step + 1, r + 1] = later(*lines[1:], r + 1)

    block = pl.ds(LEFT, COLS)
    inner = ROWS - 2 * STEPS
    zero = jnp.zeros((COLS, LEV), jnp.float32)
    with jax.named_scope("gather"):
        guess = lax.fori_loop(0, inner // 4, lambda i, v: v + sum(dt[STEPS, 2 * STEPS + 4 * i + n, block] for n in range(4)), zero) * (1.0 / inner)

        def gather(lines, totals):
            for line in lines:
                moved = line - guess
                totals = (totals[0] + moved, totals[1] + moved * moved)
            return totals

        totals = lax.fori_loop(0, inner // 2, lambda i, t: gather([dt[STEPS, 2 * STEPS + 2 * i + n, block] for n in range(2)], t), (zero, zero))

    for n, diagonals in enumerate(DIAGONALS):
        with jax.named_scope("arrive_py"):
            for a in (-1, 1):
                if n == 0:
                    for b in (-1, 1):
                        arrive(a, b)
                arrive(a, 0, slice(2 * n, 2 * n + 2))
        with jax.named_scope("outer"):
            for k in diagonals:
                up = dt[0, TOP - k]
                down = dt[0, TOP + ROWS - 1 + k]
                for t in range(STEPS):
                    r, q = TOP - k + t + 1, TOP + ROWS - 2 + k - t
                    up = later(up, dt[t, r], dt[t, r + 1], r)
                    down = later(dt[t, q - 1], dt[t, q], down, q)
                    dt[t + 1, r] = up
                    dt[t + 1, q] = down
    with jax.named_scope("part"):
        totals = gather([dt[STEPS, r, block] for n in range(STEPS) for r in (TOP + n, TOP + ROWS - 1 - n)], totals)
        offset = totals[0] * (1.0 / ROWS)
        part[0] = guess + offset
        part[1] = totals[1] - totals[0] * offset

    def send(peer, count, mine, got, sends, recvs, at):
        base = at * (count - 1)
        return [
            pltpu.make_async_remote_copy(mine, got.at[base + k - 1], sends.at[base + k - 1], recvs.at[base + k - 1], device_id=peer(k), device_id_type=MESH)
            for k in range(1, count)
        ]

    def start(copies):
        middle = len(copies) // 2
        for k in sorted(range(len(copies)), key=lambda k: abs(k - middle)):
            copies[k].start()

    def collect(copies, mine, got, at, each):
        for copy in copies:
            copy.wait_recv()
        base = at * len(copies)
        return merged(*([mine[s]] + [got[base + k, s] for k in range(len(copies))] for s in (0, 1)), each)

    halves = [part.at[:, pl.ds(h * HALF, HALF)] for h in (0, 1)]
    cells = float(ROWS)
    xa = send(xpeer, XS, halves[0], xin, xs_sem, xr_sem, 0)
    zb = send(zpeer, zs, halves[1], zin, zs_sem, zr_sem, 1)
    za = send(zpeer, zs, mid_part.at[0], zin, zs_sem, zr_sem, 0)
    xb = send(xpeer, XS, mid_part.at[1], xin, xs_sem, xr_sem, 1)
    start(xa)
    start(zb)

    @pl.loop(0, ROWS)
    def _(i):
        e_out[i] = dt[STEPS, TOP + i, block]

    with jax.named_scope("xa"):
        mid_part[0, 0], mid_part[0, 1] = collect(xa, halves[0], xin, 0, cells)
    start(za)
    with jax.named_scope("zb"):
        mid_part[1, 0], mid_part[1, 1] = collect(zb, halves[1], zin, 1, cells)
    start(xb)
    with jax.named_scope("za"):
        mean_a, spread_a = collect(za, mid_part.at[0], zin, 0, cells * XS)
        stats[0, :HALF] = mean_a
        stats[1, :HALF] = lax.rsqrt(spread_a * (1.0 / (ROWS * npy)) + EPS)
    with jax.named_scope("xb"):
        mean_b, spread_b = collect(xb, mid_part.at[1], xin, 1, cells * zs)
        stats[0, HALF:] = mean_b
        stats[1, HALF:] = lax.rsqrt(spread_b * (1.0 / (ROWS * npy)) + EPS)
    for copy in xa + xb + za + zb:
        copy.wait_send()
    for a, b in order:
        @pl.when(there(a, b))
        def _():
            for copy in halo(a, b):
                copy.wait_send()


def finish(end, stats, a_out, e_out, held, sem):
    whole = pltpu.make_async_copy(end, e_out, sem.at[0])
    whole.start()
    mean, scale = stats[0], stats[1]
    quarter = ROWS // 4
    copies = []
    for q in range(4):
        @pl.loop(q * quarter, (q + 1) * quarter)
        def _(i):
            held[i] = (end[i] - mean) * scale

        rows = pl.ds(q * quarter, quarter)
        copies.append(pltpu.make_async_copy(held.at[rows], a_out.at[rows], sem.at[1 + q]))
        copies[-1].start()
    whole.wait()
    for copy in copies:
        copy.wait()


def solution(mesh):
    npy, npx = mesh.shape["py"], mesh.shape["px"]
    zs = npy // XS

    def per_device(density, conductance, source):
        shape = jax.ShapeDtypeStruct((ROWS, COLS, LEV), jnp.float32)
        f32 = jnp.float32
        dma = pltpu.SemaphoreType.DMA
        end, stats = pl.pallas_call(
            functools.partial(kernel, npy, npx),
            name="diffuse",
            out_shape=(pltpu.VMEM((ROWS, COLS, LEV), f32), pltpu.VMEM((2, COLS, LEV), f32)),
            in_specs=[pl.BlockSpec(memory_space=pl.ANY)] * 3,
            out_specs=[pl.BlockSpec(memory_space=pltpu.VMEM)] * 2,
            scratch_shapes=[
                pltpu.VMEM((STEPS + 1, HIGH, WIDE, LEV), f32),
                pltpu.VMEM((2, HIGH, WIDE, LEV), f32),
                pltpu.VMEM((2, COLS, LEV), f32),
                pltpu.VMEM((2, 2, HALF, LEV), f32),
                pltpu.VMEM((2 * (XS - 1), 2, HALF, LEV), f32),
                pltpu.VMEM((2 * (zs - 1), 2, HALF, LEV), f32),
                dma((3,)), dma((COPIES,)), dma((COPIES,)),
                dma((2 * (XS - 1),)), dma((2 * (XS - 1),)), dma((2 * (zs - 1),)), dma((2 * (zs - 1),)),
            ],
            compiler_params=pltpu.CompilerParams(collective_id=0, has_side_effects=True),
        )(density, conductance, source)
        return pl.pallas_call(
            finish,
            name="finish",
            out_shape=(shape, shape),
            in_specs=[pl.BlockSpec(memory_space=pltpu.VMEM)] * 2,
            out_specs=[pl.BlockSpec(memory_space=pl.ANY)] * 2,
            scratch_shapes=[pltpu.VMEM((ROWS, COLS, LEV), f32), dma((5,))],
        )(*(pltpu.with_memory_space_constraint(v, pltpu.VMEM) for v in (end, stats)))

    spec = P("py", "px", None)
    return jax.shard_map(per_device, mesh=mesh, in_specs=(spec,) * 3, out_specs=(spec, spec), check_vma=False)
```

time: 33.4 us -> 30.2 us (0.904)
  Pallas kernels: 32.6 us -> 29.3 us
    pallas_call x1, Pallas kernels: 31.6 us -> 28.3 us  [per_device(): pl.pallas_call(functools.partial(kernel, npy, npx), name='diffuse', out_s...]
where the time goes in v3:
time: 30.2 us; the launch traced here: 30 us
  Pallas kernels  29.3 us (97%)
  between operations  0.64 us (2%)
    pallas_call x1, Pallas kernels, per_device(): pl.pallas_call(functools.partial(kernel, npy, npx), name='diffuse', out_s...  28.3 us
    pallas_call x1, Pallas kernels, per_device(): pl.pallas_call(finish, name='finish', out_shape=(shape, shape), in_specs=...  1 us

profile of v3, /device:TPU:8, one launch (start us, length us, event | category | flops | bytes accessed | tf_op | source)
XLA Modules:
  0.0 30.0 jit_solution(14904378243546871756)
XLA Ops:
  0.6 28.3 %diffuse.1 = (f32[32,32,128]{2,1,0:T(8,128)S(1)}, f32[2,32,128]{2,1,0:T(8,128)S(1)}) custom-call(f32[32,32,128]{2,1,0:T(8,128)} %d_hbm.1, f32[32,32,128]{2,1,0:T(8,128)} %c_hbm.1, f32[32,32,128]{2,1,0:T(8,128)} %s_hbm.1), custom_call_target="tpu_custom_call" | custom-call | tf_op jit(solution)/shard_map/diffuse/pallas_call | solution.py:287
  29.0 1.0 %finish.1 = (f32[32,32,128]{2,1,0:T(8,128)}, f32[32,32,128]{2,1,0:T(8,128)}) custom-call(f32[32,32,128]{2,1,0:T(8,128)S(1)} %get-tuple-element.4.end, f32[2,32,128]{2,1,0:T(8,128)S(1)} %get-tuple-element.5.stats), custom_call_target="tpu_custom_call" | custom-call | tf_op jit(solution)/shard_map/finish/pallas_call | solution.py:305

commit v4 on v3

v4 whole, which is shorter than its diff:
```python
import functools

import jax
import jax.numpy as jnp
from jax import lax
from jax.experimental import pallas as pl
from jax.experimental.pallas import tpu as pltpu
from jax.sharding import PartitionSpec as P

STEPS = 6
EPS = 1e-4
XS = 4
ROWS, COLS, LEV = 32, 32, 128
TOP, LEFT = STEPS, 8
HIGH, WIDE = ROWS + 2 * STEPS, COLS + 2 * LEFT
HALF = COLS // 2
MESH = pl.DeviceIdType.MESH
SIDES = [(a, b) for a in (-1, 0, 1) for b in (-1, 0, 1) if a or b]
SKY, LATE = 4, 2
FIELD, COEF, AHEAD = 0, 1, 2
DIAGONALS = ((1, 2, 3), (4,), (5, 6))


def reach(side, size, start, first, last):
    length = last - first + 1
    if side > 0:
        return pl.ds(start + size - last, length), pl.ds(start - last, length)
    return pl.ds(start + first - 1, length), pl.ds(start + size + first - 1, length)


def halo_groups(a, b):
    def to(which, rows, cols):
        (fr, tr), (fc, tc) = rows, cols
        return which, (fr, fc), (tr, tc), fr.size * fc.size * (2 if which == COEF else 1)

    def rows_of(first, last):
        return reach(a, ROWS, TOP, first, last)

    def cols_of(first, last):
        return reach(b, COLS, LEFT, first, last)

    def same(start, size):
        return pl.ds(start, size), pl.ds(start, size)

    whole = same(LEFT, COLS)
    if a and b:
        return [[
            to(FIELD, rows_of(1, 2), cols_of(1, 5)), to(FIELD, rows_of(3, 5), cols_of(1, 3)),
            to(COEF, rows_of(1, 2), cols_of(1, 4)), to(COEF, rows_of(3, 4), cols_of(1, 2)),
        ]]
    if b:
        return [[to(FIELD, same(TOP, ROWS), cols_of(1, STEPS)), to(COEF, same(TOP, ROWS), cols_of(1, STEPS - 1))]]
    edges = []
    for left in (True, False):
        edges.append(to(FIELD, rows_of(5, 6), same(LEFT if left else LEFT + COLS - 3, 3)))
        edges.append(to(COEF, rows_of(4, 5), same(LEFT if left else LEFT + COLS - 2, 2)))
    side = same(0, LATE)
    return [
        [to(FIELD, rows_of(1, 3), whole), to(COEF, rows_of(1, 2), whole)],
        [to(FIELD, rows_of(4, 4), whole), to(COEF, rows_of(3, 3), whole)],
        edges + [to(AHEAD, side, same(0, COLS))],
    ]


GROUPS = {side: halo_groups(*side) for side in SIDES}
BASE = {}
for _side in SIDES:
    BASE[_side] = sum(len(GROUPS[s]) for s in BASE)
COPIES = sum(len(g) for g in GROUPS.values())


def area(cells):
    for rows in range(1, HIGH + 1):
        if cells % rows == 0 and cells // rows <= WIDE:
            return pl.ds(0, rows), pl.ds(0, cells // rows)
    raise ValueError(cells)


def merged(means, spreads, each):
    mean = sum(means[1:], means[0]) * (1.0 / len(means))
    spread = sum(spreads[1:], spreads[0])
    for m in means:
        spread = spread + each * (m - mean) * (m - mean)
    return mean, spread


def kernel(npy, npx, d_hbm, c_hbm, s_hbm, e_out, stats, dt, cs, sky, ahead, part, mid_part, xin, zin,
           load_sem, hs_sem, hr_sem, ts_sem, tr_sem, token):
    py, px = lax.axis_index("py"), lax.axis_index("px")
    zs = npy // XS
    z, x = py // XS, lax.rem(py, XS)
    rounds = 0
    while 2 ** rounds < zs // 2:
        rounds += 1
    own = (pl.ds(TOP, ROWS), pl.ds(LEFT, COLS))

    def there(a, b):
        ok = None
        for side, at, count in ((a, py, npy), (b, px, npx)):
            if side:
                good = (at < count - 1) if side > 0 else (at > 0)
                ok = good if ok is None else ok & good
        return ok

    def xpeer(k):
        return {"py": z * XS + lax.rem(x + k, XS), "px": px}

    def zpeer(k):
        return {"py": lax.rem(z + k, zs) * XS + x, "px": px}

    barrier = pltpu.get_barrier_semaphore()
    for a, b in SIDES:
        @pl.when(there(a, b))
        def _():
            pl.semaphore_signal(barrier, inc=1, device_id={"py": py + a, "px": px + b}, device_id_type=MESH)
    for k in range(1, XS):
        pl.semaphore_signal(barrier, inc=1, device_id=xpeer(k), device_id_type=MESH)
    beyond = sorted({1, zs - 1})
    for k in beyond:
        pl.semaphore_signal(barrier, inc=1, device_id=zpeer(k), device_id_type=MESH)

    loads = [
        pltpu.make_async_copy(d_hbm, dt.at[(0, *own)], load_sem.at[0]),
        pltpu.make_async_copy(c_hbm, cs.at[(0, *own)], load_sem.at[1]),
        pltpu.make_async_copy(s_hbm, cs.at[(1, *own)], load_sem.at[2]),
    ]
    for load in loads:
        load.start()

    for a in (-1, 1):
        @pl.when(jnp.logical_not(there(a, 0)))
        def _():
            rows = pl.ds(0, TOP) if a < 0 else pl.ds(TOP + ROWS, STEPS)
            dt[0, rows] = jnp.zeros((STEPS, WIDE, LEV), jnp.float32)
            cs[:, rows] = jnp.zeros((2, STEPS, WIDE, LEV), jnp.float32)
            sky[(a + 1) // 2] = jnp.zeros((LATE, COLS, LEV), jnp.float32)
    for b in (-1, 1):
        @pl.when(jnp.logical_not(there(0, b)))
        def _():
            cols = pl.ds(0, LEFT) if b < 0 else pl.ds(LEFT + COLS, LEFT)
            dt[0, :, cols] = jnp.zeros((HIGH, LEFT, LEV), jnp.float32)
            cs[:, :, cols] = jnp.zeros((2, HIGH, LEFT, LEV), jnp.float32)

    with jax.named_scope("loads"):
        for load in loads:
            load.wait()
    block = pl.ds(LEFT, COLS)

    def later(above, mid, below, r, cols=slice(None)):
        width = mid.shape[0]
        spread = (above + below) + (pltpu.roll(mid, 1, 0) + pltpu.roll(mid, width - 1, 0)) - 4.0 * mid
        return mid + cs[0, r, cols] * spread + cs[1, r, cols]

    for a in (-1, 1):
        lines = {}
        for off in range(-LATE, LATE + 1):
            r = (TOP + SKY - 1 if a < 0 else TOP + ROWS - SKY) + off
            lines[r] = dt[0, r, block]
        for level in range(LATE):
            lines = {r: later(lines[r - 1], lines[r], lines[r + 1], r, block) for r in lines if r - 1 in lines and r + 1 in lines}
            ahead[(a + 1) // 2, level] = lines[TOP + SKY - 1 if a < 0 else TOP + ROWS - SKY]

    near = (py > 0).astype(jnp.int32) + (py < npy - 1).astype(jnp.int32)
    beside = (px > 0).astype(jnp.int32) + (px < npx - 1).astype(jnp.int32)
    with jax.named_scope("barrier"):
        pl.semaphore_wait(barrier, (near + 1) * (beside + 1) - 1 + XS - 1 + len(beyond))

    def tell(n, away):
        for k in (away, zs - away):
            pl.semaphore_signal(token.at[n], inc=1, device_id=zpeer(k), device_id_type=MESH)

    if rounds:
        tell(0, 1)

    def halo(a, b, group):
        to = {"py": py + a, "px": px + b}
        at = BASE[a, b] + group
        copies = []
        for which, source, target, _ in GROUPS[a, b][group]:
            if which == COEF:
                src, dst = cs.at[(slice(None), *source)], cs.at[(slice(None), *target)]
            elif which == FIELD:
                src, dst = dt.at[(0, *source)], dt.at[(0, *target)]
            else:
                src, dst = ahead.at[(a + 1) // 2], sky.at[(1 - a) // 2]
            copies.append(pltpu.make_async_remote_copy(src, dst, hs_sem.at[at], hr_sem.at[at], device_id=to, device_id_type=MESH))
        return copies

    def all_of(a, b, group, sems):
        rows, cols = area(sum(copy[3] for copy in GROUPS[a, b][group]))
        cells = dt.at[0, rows, cols]
        pltpu.make_async_copy(cells, cells, sems.at[BASE[a, b] + group]).wait()

    order = [(0, 1), (0, -1)] + [(a, b) for a, b in SIDES if a and b]
    order = [(*side, 0) for side in order] + [(a, 0, n) for n in range(3) for a in (1, -1)]
    with jax.named_scope("sends"):
        for a, b, n in order:
            @pl.when(there(a, b))
            def _():
                for copy in halo(a, b, n):
                    copy.start()

    def arrive(a, b, n=0):
        @pl.when(there(a, b))
        def _():
            all_of(-a, -b, n, hr_sem)

    def inner(first, last, low, high):
        read, kept = pl.ds(8 * first, 8 * (last - first)), pl.ds(8 * low, 8 * (high - low))
        cut = slice(8 * (low - first), 8 * (high - first))

        def line(step, above, mid, below, r):
            side = (pltpu.roll(mid, 1, 0) + pltpu.roll(mid, mid.shape[0] - 1, 0))[cut]
            mid = mid[cut]
            dt[step + 1, r, kept] = mid + cs[0, r, kept] * ((above + below) + side - 4.0 * mid) + cs[1, r, kept]

        for step in range(STEPS):
            start, count = TOP + step + 1, ROWS - 2 * (step + 1)

            @pl.loop(0, count // 2)
            def _(i):
                r = start + 2 * i
                one, two = dt[step, r, read], dt[step, r + 1, read]
                line(step, dt[step, r - 1, kept], one, two[cut], r)
                line(step, one[cut], two, dt[step, r + 2, kept], r + 1)

    with jax.named_scope("own_cols"):
        inner(1, 5, 1, 5)
    with jax.named_scope("arrive_px"):
        arrive(0, -1)
        arrive(0, 1)
    if rounds:
        with jax.named_scope("token"):
            pl.semaphore_wait(token.at[0], 2)
        if rounds > 1:
            tell(1, 2)
    with jax.named_scope("inner"):
        inner(0, 3, 0, 2)
        inner(3, 6, 4, 6)
    far = ROWS - 2 * STEPS
    zero = jnp.zeros((COLS, LEV), jnp.float32)
    place = lax.broadcasted_iota(jnp.int32, (WIDE, LEV), 0) - LEFT

    def outer(k):
        up = dt[0, TOP - k]
        down = dt[0, TOP + ROWS - 1 + k]
        for t in range(STEPS):
            r, q = TOP - k + t + 1, TOP + ROWS - 2 + k - t
            up = later(up, dt[t, r], dt[t, r + 1], r)
            down = later(dt[t, q - 1], dt[t, q], down, q)
            if k == SKY + t + 1:
                known = (place > t) & (place < COLS - 1 - t)
                edge = jnp.zeros((LEFT, LEV), jnp.float32)
                up, down = (jnp.where(known, jnp.concatenate([edge, sky[side, t], edge], axis=0), new) for side, new in ((0, up), (1, down)))
            dt[t + 1, r] = up
            dt[t + 1, q] = down

    def come(n):
        with jax.named_scope("arrive_py"):
            for a in (-1, 1):
                if n == 0:
                    for b in (-1, 1):
                        arrive(a, b)
                arrive(a, 0, n)
        with jax.named_scope("outer"):
            for k in DIAGONALS[n]:
                outer(k)

    come(0)
    with jax.named_scope("gather"):
        guess = lax.fori_loop(0, far // 4, lambda i, v: v + sum(dt[STEPS, 2 * STEPS + 4 * i + n, block] for n in range(4)), zero) * (1.0 / far)

        def gather(lines, totals):
            for line in lines:
                moved = line - guess
                totals = (totals[0] + moved, totals[1] + moved * moved)
            return totals

        totals = lax.fori_loop(0, far // 2, lambda i, t: gather([dt[STEPS, 2 * STEPS + 2 * i + n, block] for n in range(2)], t), (zero, zero))

    come(1)
    come(2)
    with jax.named_scope("part"):
        totals = gather([dt[STEPS, r, block] for n in range(STEPS) for r in (TOP + n, TOP + ROWS - 1 - n)], totals)
        offset = totals[0] * (1.0 / ROWS)
        part[0] = guess + offset
        part[1] = totals[1] - totals[0] * offset

    def send(peer, count, mine, got, phase):
        base = 0 if phase in (0, 3) else count - 1
        return [
            pltpu.make_async_remote_copy(mine, got.at[base + k - 1], ts_sem.at[phase], tr_sem.at[phase], device_id=peer(k), device_id_type=MESH)
            for k in range(1, count)
        ]

    def start(copies):
        middle = len(copies) // 2
        for k in sorted(range(len(copies)), key=lambda k: abs(k - middle)):
            copies[k].start()

    def done(got, count, phase, sems):
        base = 0 if phase in (0, 3) else count - 1
        cells = got.at[pl.ds(base, count - 1)]
        pltpu.make_async_copy(cells, cells, sems.at[phase]).wait()

    def collect(mine, got, count, phase, each):
        done(got, count, phase, tr_sem)
        base = 0 if phase in (0, 3) else count - 1
        return merged(*([mine[s]] + [got[base + k, s] for k in range(count - 1)] for s in (0, 1)), each)

    halves = [part.at[:, pl.ds(h * HALF, HALF)] for h in (0, 1)]
    cells = float(ROWS)
    xa = send(xpeer, XS, halves[0], xin, 0)
    zb = send(zpeer, zs, halves[1], zin, 1)
    xb = send(xpeer, XS, mid_part.at[1], xin, 2)
    za = send(zpeer, zs, mid_part.at[0], zin, 3)
    start(xa)
    for n in range(1, rounds):
        with jax.named_scope("token"):
            pl.semaphore_wait(token.at[n], 2)
        if n + 1 < rounds:
            tell(n + 1, 2 ** (n + 1))
    start(zb)

    @pl.loop(0, ROWS)
    def _(i):
        e_out[i] = dt[STEPS, TOP + i, block]

    for a, b, n in order:
        @pl.when(there(a, b))
        def _():
            all_of(a, b, n, hs_sem)

    with jax.named_scope("xa"):
        mid_part[0, 0], mid_part[0, 1] = collect(halves[0], xin, XS, 0, cells)
    start(za)
    with jax.named_scope("zb"):
        mid_part[1, 0], mid_part[1, 1] = collect(halves[1], zin, zs, 1, cells)
    start(xb)
    with jax.named_scope("za"):
        mean_a, spread_a = collect(mid_part.at[0], zin, zs, 3, cells * XS)
        stats[0, :HALF] = mean_a
        stats[1, :HALF] = lax.rsqrt(spread_a * (1.0 / (ROWS * npy)) + EPS)
    with jax.named_scope("xb"):
        mean_b, spread_b = collect(mid_part.at[1], xin, XS, 2, cells * zs)
        stats[0, HALF:] = mean_b
        stats[1, HALF:] = lax.rsqrt(spread_b * (1.0 / (ROWS * npy)) + EPS)
    for got, count, phase in ((xin, XS, 0), (zin, zs, 1), (xin, XS, 2), (zin, zs, 3)):
        done(got, count, phase, ts_sem)


def finish(end, stats, a_out, e_out, held, sem):
    whole = pltpu.make_async_copy(end, e_out, sem.at[0])
    whole.start()
    mean, scale = stats[0], stats[1]
    quarter = ROWS // 4
    copies = []
    for q in range(4):
        @pl.loop(q * quarter, (q + 1) * quarter)
        def _(i):
            held[i] = (end[i] - mean) * scale

        rows = pl.ds(q * quarter, quarter)
        copies.append(pltpu.make_async_copy(held.at[rows], a_out.at[rows], sem.at[1 + q]))
        copies[-1].start()
    whole.wait()
    for copy in copies:
        copy.wait()


def solution(mesh):
    npy, npx = mesh.shape["py"], mesh.shape["px"]
    zs = npy // XS

    def per_device(density, conductance, source):
        shape = jax.ShapeDtypeStruct((ROWS, COLS, LEV), jnp.float32)
        f32 = jnp.float32
        dma = pltpu.SemaphoreType.DMA
        end, stats = pl.pallas_call(
            functools.partial(kernel, npy, npx),
            name="diffuse",
            out_shape=(pltpu.VMEM((ROWS, COLS, LEV), f32), pltpu.VMEM((2, COLS, LEV), f32)),
            in_specs=[pl.BlockSpec(memory_space=pl.ANY)] * 3,
            out_specs=[pl.BlockSpec(memory_space=pltpu.VMEM)] * 2,
            scratch_shapes=[
                pltpu.VMEM((STEPS + 1, HIGH, WIDE, LEV), f32),
                pltpu.VMEM((2, HIGH, WIDE, LEV), f32),
                pltpu.VMEM((2, LATE, COLS, LEV), f32),
                pltpu.VMEM((2, LATE, COLS, LEV), f32),
                pltpu.VMEM((2, COLS, LEV), f32),
                pltpu.VMEM((2, 2, HALF, LEV), f32),
                pltpu.VMEM((2 * (XS - 1), 2, HALF, LEV), f32),
                pltpu.VMEM((2 * (zs - 1), 2, HALF, LEV), f32),
                dma((3,)), dma((COPIES,)), dma((COPIES,)),
                dma((4,)), dma((4,)), pltpu.SemaphoreType.REGULAR((2,)),
            ],
            compiler_params=pltpu.CompilerParams(collective_id=0, has_side_effects=True),
        )(density, conductance, source)
        return pl.pallas_call(
            finish,
            name="finish",
            out_shape=(shape, shape),
            in_specs=[pl.BlockSpec(memory_space=pltpu.VMEM)] * 2,
            out_specs=[pl.BlockSpec(memory_space=pl.ANY)] * 2,
            scratch_shapes=[pltpu.VMEM((ROWS, COLS, LEV), f32), dma((5,))],
        )(*(pltpu.with_memory_space_constraint(v, pltpu.VMEM) for v in (end, stats)))

    spec = P("py", "px", None)
    return jax.shard_map(per_device, mesh=mesh, in_specs=(spec,) * 3, out_specs=(spec, spec), check_vma=False)
```

time: 30.2 us -> 28.1 us (0.930); the launches traced: 30 us -> 27.6 us
  Pallas kernels: 29.3 us -> 26.9 us
    pallas_call x1, Pallas kernels: 28.3 us -> 25.9 us  [per_device(): pl.pallas_call(functools.partial(kernel, npy, npx), name='diffuse', out_s...]
where the time goes in v4:
time: 28.1 us; the launch traced here: 27.6 us
  Pallas kernels  26.9 us (96%)
  between operations  0.64 us (2%)
    pallas_call x1, Pallas kernels, per_device(): pl.pallas_call(functools.partial(kernel, npy, npx), name='diffuse', out_s...  25.9 us
    pallas_call x1, Pallas kernels, per_device(): pl.pallas_call(finish, name='finish', out_shape=(shape, shape), in_specs=...  1 us

profile of v4, /device:TPU:8, one launch (start us, length us, event | category | flops | bytes accessed | tf_op | source)
XLA Modules:
  0.0 27.6 jit_solution(1600501279935981068)
XLA Ops:
  0.6 25.9 %diffuse.1 = (f32[32,32,128]{2,1,0:T(8,128)S(1)}, f32[2,32,128]{2,1,0:T(8,128)S(1)}) custom-call(f32[32,32,128]{2,1,0:T(8,128)} %d_hbm.1, f32[32,32,128]{2,1,0:T(8,128)} %c_hbm.1, f32[32,32,128]{2,1,0:T(8,128)} %s_hbm.1), custom_call_target="tpu_custom_call" | custom-call | tf_op jit(solution)/shard_map/diffuse/pallas_call | solution.py:379
  26.6 1.0 %finish.1 = (f32[32,32,128]{2,1,0:T(8,128)}, f32[32,32,128]{2,1,0:T(8,128)}) custom-call(f32[32,32,128]{2,1,0:T(8,128)S(1)} %get-tuple-element.4.end, f32[2,32,128]{2,1,0:T(8,128)S(1)} %get-tuple-element.5.stats), custom_call_target="tpu_custom_call" | custom-call | tf_op jit(solution)/shard_map/finish/pallas_call | solution.py:399

commit v5 on v4

--- a/solution.py
+++ b/solution.py
@@ -14,6 +14,8 @@
 TOP, LEFT = STEPS, 8
 HIGH, WIDE = ROWS + 2 * STEPS, COLS + 2 * LEFT
 HALF = COLS // 2
+ROWS_OWN, ROWS_SIDE = 6, 6
+NEAR_FAR = ((0, 1), (2,))
 MESH = pl.DeviceIdType.MESH
 SIDES = [(a, b) for a in (-1, 0, 1) for b in (-1, 0, 1) if a or b]
 SKY, LATE = 4, 2
@@ -62,6 +64,8 @@
     ]
 
 
+NEXT = [(a, b) for a, b in SIDES if not (a and b)]
+CORNERS = [(a, b) for a, b in SIDES if a and b]
 GROUPS = {side: halo_groups(*side) for side in SIDES}
 BASE = {}
 for _side in SIDES:
@@ -85,15 +89,13 @@
 
 
 def kernel(npy, npx, d_hbm, c_hbm, s_hbm, e_out, stats, dt, cs, sky, ahead, part, mid_part, xin, zin,
-           load_sem, hs_sem, hr_sem, ts_sem, tr_sem, token):
+           load_sem, hs_sem, hr_sem, ts_sem, tr_sem, token, met):
     py, px = lax.axis_index("py"), lax.axis_index("px")
     zs = npy // XS
     z, x = py // XS, lax.rem(py, XS)
     rounds = 0
     while 2 ** rounds < zs // 2:
         rounds += 1
-    own = (pl.ds(TOP, ROWS), pl.ds(LEFT, COLS))
-
     def there(a, b):
         ok = None
         for side, at, count in ((a, py, npy), (b, px, npx)):
@@ -108,8 +110,21 @@
     def zpeer(k):
         return {"py": lax.rem(z + k, zs) * XS + x, "px": px}
 
+    def loads(first, count, sem):
+        rows, cols = pl.ds(TOP + first, count), pl.ds(LEFT, COLS)
+        return [
+            pltpu.make_async_copy(hbm.at[pl.ds(first, count)], to.at[field, rows, cols], load_sem.at[sem])
+            for hbm, to, field in ((d_hbm, dt, 0), (c_hbm, cs, 0), (s_hbm, cs, 1))
+        ]
+
+    def loaded(count, sem):
+        cells = dt.at[pl.ds(0, 3), pl.ds(0, count), pl.ds(LEFT, COLS)]
+        pltpu.make_async_copy(cells, cells, load_sem.at[sem]).wait()
+
+    for load in loads(0, STEPS, 0) + loads(ROWS - STEPS, STEPS, 0):
+        load.start()
     barrier = pltpu.get_barrier_semaphore()
-    for a, b in SIDES:
+    for a, b in NEXT:
         @pl.when(there(a, b))
         def _():
             pl.semaphore_signal(barrier, inc=1, device_id={"py": py + a, "px": px + b}, device_id_type=MESH)
@@ -119,12 +134,7 @@
     for k in beyond:
         pl.semaphore_signal(barrier, inc=1, device_id=zpeer(k), device_id_type=MESH)
 
-    loads = [
-        pltpu.make_async_copy(d_hbm, dt.at[(0, *own)], load_sem.at[0]),
-        pltpu.make_async_copy(c_hbm, cs.at[(0, *own)], load_sem.at[1]),
-        pltpu.make_async_copy(s_hbm, cs.at[(1, *own)], load_sem.at[2]),
-    ]
-    for load in loads:
+    for load in loads(STEPS, ROWS - 2 * STEPS, 1):
         load.start()
 
     for a in (-1, 1):
@@ -142,8 +152,7 @@
             cs[:, :, cols] = jnp.zeros((2, HIGH, LEFT, LEV), jnp.float32)
 
     with jax.named_scope("loads"):
-        for load in loads:
-            load.wait()
+        loaded(2 * STEPS, 0)
     block = pl.ds(LEFT, COLS)
 
     def later(above, mid, below, r, cols=slice(None)):
@@ -163,7 +172,7 @@
     near = (py > 0).astype(jnp.int32) + (py < npy - 1).astype(jnp.int32)
     beside = (px > 0).astype(jnp.int32) + (px < npx - 1).astype(jnp.int32)
     with jax.named_scope("barrier"):
-        pl.semaphore_wait(barrier, (near + 1) * (beside + 1) - 1 + XS - 1 + len(beyond))
+        pl.semaphore_wait(barrier, near + beside + XS - 1 + len(beyond))
 
     def tell(n, away):
         for k in (away, zs - away):
@@ -171,6 +180,10 @@
 
     if rounds:
         tell(0, 1)
+    for b in (-1, 1):
+        @pl.when(there(0, b))
+        def _():
+            pl.semaphore_signal(met, inc=1, device_id={"py": py, "px": px + b}, device_id_type=MESH)
 
     def halo(a, b, group):
         to = {"py": py + a, "px": px + b}
@@ -191,41 +204,56 @@
         cells = dt.at[0, rows, cols]
         pltpu.make_async_copy(cells, cells, sems.at[BASE[a, b] + group]).wait()
 
-    order = [(0, 1), (0, -1)] + [(a, b) for a, b in SIDES if a and b]
-    order = [(*side, 0) for side in order] + [(a, 0, n) for n in range(3) for a in (1, -1)]
-    with jax.named_scope("sends"):
-        for a, b, n in order:
+    beside_sends = [(0, 1, 0), (0, -1, 0)]
+    corner_sends = [(a, b, 0) for a, b in CORNERS]
+    near_sends, far_sends = ([(a, 0, n) for n in groups for a in (1, -1)] for groups in NEAR_FAR)
+
+    def send_halo(sends):
+        for a, b, n in sends:
             @pl.when(there(a, b))
             def _():
                 for copy in halo(a, b, n):
                     copy.start()
 
+    with jax.named_scope("sends"):
+        send_halo(near_sends)
+
+    with jax.named_scope("loads2"):
+        loaded(ROWS - 2 * STEPS, 1)
+    send_halo(beside_sends)
+
     def arrive(a, b, n=0):
         @pl.when(there(a, b))
         def _():
             all_of(-a, -b, n, hr_sem)
 
-    def inner(first, last, low, high):
-        read, kept = pl.ds(8 * first, 8 * (last - first)), pl.ds(8 * low, 8 * (high - low))
-        cut = slice(8 * (low - first), 8 * (high - first))
-
-        def line(step, above, mid, below, r):
-            side = (pltpu.roll(mid, 1, 0) + pltpu.roll(mid, mid.shape[0] - 1, 0))[cut]
-            mid = mid[cut]
-            dt[step + 1, r, kept] = mid + cs[0, r, kept] * ((above + below) + side - 4.0 * mid) + cs[1, r, kept]
+    def inner(strips, rows):
+        def lines(step, r, first, last, low, high):
+            read, kept = pl.ds(8 * first, 8 * (last - first)), pl.ds(8 * low, 8 * (high - low))
+            cut = slice(8 * (low - first), 8 * (high - first))
+            held = [dt[step, r + n, read] for n in range(rows)]
+            cuts = [dt[step, r - 1, kept]] + [h[cut] for h in held] + [dt[step, r + rows, kept]]
+            for n, mid in enumerate(held):
+                side = (pltpu.roll(mid, 1, 0) + pltpu.roll(mid, mid.shape[0] - 1, 0))[cut]
+                spread = (cuts[n] + cuts[n + 2]) + side - 4.0 * cuts[n + 1]
+                dt[step + 1, r + n, kept] = cuts[n + 1] + cs[0, r + n, kept] * spread + cs[1, r + n, kept]
 
         for step in range(STEPS):
             start, count = TOP + step + 1, ROWS - 2 * (step + 1)
 
-            @pl.loop(0, count // 2)
+            @pl.loop(0, pl.cdiv(count, rows))
             def _(i):
-                r = start + 2 * i
-                one, two = dt[step, r, read], dt[step, r + 1, read]
-                line(step, dt[step, r - 1, kept], one, two[cut], r)
-                line(step, one[cut], two, dt[step, r + 2, kept], r + 1)
+                r = start + jnp.minimum(rows * i, count - rows)
+                for strip in strips:
+                    lines(step, r, *strip)
 
     with jax.named_scope("own_cols"):
-        inner(1, 5, 1, 5)
+        inner(((1, 5, 1, 5),), ROWS_OWN)
+    with jax.named_scope("met"):
+        pl.semaphore_wait(met, beside)
+    send_halo(corner_sends)
+
+    send_halo(far_sends)
     with jax.named_scope("arrive_px"):
         arrive(0, -1)
         arrive(0, 1)
@@ -235,8 +263,7 @@
         if rounds > 1:
             tell(1, 2)
     with jax.named_scope("inner"):
-        inner(0, 3, 0, 2)
-        inner(3, 6, 4, 6)
+        inner(((0, 3, 0, 2), (3, 6, 4, 6)), ROWS_SIDE)
     far = ROWS - 2 * STEPS
     zero = jnp.zeros((COLS, LEV), jnp.float32)
     place = lax.broadcasted_iota(jnp.int32, (WIDE, LEV), 0) - LEFT
@@ -326,7 +353,7 @@
     def _(i):
         e_out[i] = dt[STEPS, TOP + i, block]
 
-    for a, b, n in order:
+    for a, b, n in beside_sends + corner_sends + near_sends + far_sends:
         @pl.when(there(a, b))
         def _():
             all_of(a, b, n, hs_sem)
@@ -391,8 +418,8 @@
                 pltpu.VMEM((2, 2, HALF, LEV), f32),
                 pltpu.VMEM((2 * (XS - 1), 2, HALF, LEV), f32),
                 pltpu.VMEM((2 * (zs - 1), 2, HALF, LEV), f32),
-                dma((3,)), dma((COPIES,)), dma((COPIES,)),
-                dma((4,)), dma((4,)), pltpu.SemaphoreType.REGULAR((2,)),
+                dma((2,)), dma((COPIES,)), dma((COPIES,)),
+                dma((4,)), dma((4,)), pltpu.SemaphoreType.REGULAR((2,)), pltpu.SemaphoreType.REGULAR,
             ],
             compiler_params=pltpu.CompilerParams(collective_id=0, has_side_effects=True),
         )(density, conductance, source)

time: 28.1 us -> 27.4 us (0.975); the launches traced: 27.6 us -> 27.3 us
  no operation moved by 1% of the time
where the time goes in v5:
time: 27.4 us; the launch traced here: 27.3 us
  Pallas kernels  26.7 us (97%)
  between operations  0.64 us (2%)
    pallas_call x1, Pallas kernels, per_device(): pl.pallas_call(functools.partial(kernel, npy, npx), name='diffuse', out_s...  25.7 us
    pallas_call x1, Pallas kernels, per_device(): pl.pallas_call(finish, name='finish', out_shape=(shape, shape), in_specs=...  1 us

profile of v5, /device:TPU:8, one launch (start us, length us, event | category | flops | bytes accessed | tf_op | source)
XLA Modules:
  0.0 27.3 jit_solution(3893116813252461007)
XLA Ops:
  0.6 25.7 %diffuse.1 = (f32[32,32,128]{2,1,0:T(8,128)S(1)}, f32[2,32,128]{2,1,0:T(8,128)S(1)}) custom-call(f32[32,32,128]{2,1,0:T(8,128)} %d_hbm.1, f32[32,32,128]{2,1,0:T(8,128)} %c_hbm.1, f32[32,32,128]{2,1,0:T(8,128)} %s_hbm.1), custom_call_target="tpu_custom_call" | custom-call | tf_op jit(solution)/shard_map/diffuse/pallas_call | solution.py:406
  26.3 1.0 %finish.1 = (f32[32,32,128]{2,1,0:T(8,128)}, f32[32,32,128]{2,1,0:T(8,128)}) custom-call(f32[32,32,128]{2,1,0:T(8,128)S(1)} %get-tuple-element.4.end, f32[2,32,128]{2,1,0:T(8,128)S(1)} %get-tuple-element.5.stats), custom_call_target="tpu_custom_call" | custom-call | tf_op jit(solution)/shard_map/finish/pallas_call | solution.py:426

commit v6 on v5

--- a/solution.py
+++ b/solution.py
@@ -15,6 +15,7 @@
 HIGH, WIDE = ROWS + 2 * STEPS, COLS + 2 * LEFT
 HALF = COLS // 2
 ROWS_OWN, ROWS_SIDE = 6, 6
+X_ORDER = (0, 1, 3, 2)
 NEAR_FAR = ((0, 1), (2,))
 MESH = pl.DeviceIdType.MESH
 SIDES = [(a, b) for a in (-1, 0, 1) for b in (-1, 0, 1) if a or b]
@@ -313,17 +314,15 @@
         part[0] = guess + offset
         part[1] = totals[1] - totals[0] * offset
 
-    def send(peer, count, mine, got, phase):
-        base = 0 if phase in (0, 3) else count - 1
-        return [
-            pltpu.make_async_remote_copy(mine, got.at[base + k - 1], ts_sem.at[phase], tr_sem.at[phase], device_id=peer(k), device_id_type=MESH)
-            for k in range(1, count)
-        ]
-
-    def start(copies):
-        middle = len(copies) // 2
-        for k in sorted(range(len(copies)), key=lambda k: abs(k - middle)):
-            copies[k].start()
+    def start(mine, got, count, phase, targets):
+        along_x = count == XS
+        base, here = (0 if phase in (0, 3) else count - 1), (x if along_x else z)
+        for target in targets:
+            @pl.when(here != target)
+            def _():
+                at = base + lax.rem(target - here + count, count) - 1
+                to = z * XS + target if along_x else target * XS + x
+                pltpu.make_async_remote_copy(mine, got.at[at], ts_sem.at[phase], tr_sem.at[phase], device_id={"py": to, "px": px}, device_id_type=MESH).start()
 
     def done(got, count, phase, sems):
         base = 0 if phase in (0, 3) else count - 1
@@ -337,17 +336,13 @@
 
     halves = [part.at[:, pl.ds(h * HALF, HALF)] for h in (0, 1)]
     cells = float(ROWS)
-    xa = send(xpeer, XS, halves[0], xin, 0)
-    zb = send(zpeer, zs, halves[1], zin, 1)
-    xb = send(xpeer, XS, mid_part.at[1], xin, 2)
-    za = send(zpeer, zs, mid_part.at[0], zin, 3)
-    start(xa)
+    start(halves[0], xin, XS, 0, X_ORDER)
     for n in range(1, rounds):
         with jax.named_scope("token"):
             pl.semaphore_wait(token.at[n], 2)
         if n + 1 < rounds:
             tell(n + 1, 2 ** (n + 1))
-    start(zb)
+    start(halves[1], zin, zs, 1, range(zs))
 
     @pl.loop(0, ROWS)
     def _(i):
@@ -360,10 +355,10 @@
 
     with jax.named_scope("xa"):
         mid_part[0, 0], mid_part[0, 1] = collect(halves[0], xin, XS, 0, cells)
-    start(za)
+    start(mid_part.at[0], zin, zs, 3, range(zs))
     with jax.named_scope("zb"):
         mid_part[1, 0], mid_part[1, 1] = collect(halves[1], zin, zs, 1, cells)
-    start(xb)
+    start(mid_part.at[1], xin, XS, 2, X_ORDER)
     with jax.named_scope("za"):
         mean_a, spread_a = collect(mid_part.at[0], zin, zs, 3, cells * XS)
         stats[0, :HALF] = mean_a

time: 27.4 us -> 26.5 us (0.967)
  Pallas kernels: 26.7 us -> 25.6 us
    pallas_call x1, Pallas kernels: 25.7 us -> 24.6 us  [per_device(): pl.pallas_call(functools.partial(kernel, npy, npx), name='diffuse', out_s...]
where the time goes in v6:
time: 26.5 us; the launch traced here: 26.2 us
  Pallas kernels  25.6 us (97%)
  between operations  0.64 us (2%)
    pallas_call x1, Pallas kernels, per_device(): pl.pallas_call(functools.partial(kernel, npy, npx), name='diffuse', out_s...  24.6 us
    pallas_call x1, Pallas kernels, per_device(): pl.pallas_call(finish, name='finish', out_shape=(shape, shape), in_specs=...  1 us

profile of v6, /device:TPU:8, one launch (start us, length us, event | category | flops | bytes accessed | tf_op | source)
XLA Modules:
  0.0 26.2 jit_solution(584043859985342866)
XLA Ops:
  0.6 24.6 %diffuse.1 = (f32[32,32,128]{2,1,0:T(8,128)S(1)}, f32[2,32,128]{2,1,0:T(8,128)S(1)}) custom-call(f32[32,32,128]{2,1,0:T(8,128)} %d_hbm.1, f32[32,32,128]{2,1,0:T(8,128)} %c_hbm.1, f32[32,32,128]{2,1,0:T(8,128)} %s_hbm.1), custom_call_target="tpu_custom_call" | custom-call | tf_op jit(solution)/shard_map/diffuse/pallas_call | solution.py:401
  25.2 1.0 %finish.1 = (f32[32,32,128]{2,1,0:T(8,128)}, f32[32,32,128]{2,1,0:T(8,128)}) custom-call(f32[32,32,128]{2,1,0:T(8,128)S(1)} %get-tuple-element.4.end, f32[2,32,128]{2,1,0:T(8,128)S(1)} %get-tuple-element.5.stats), custom_call_target="tpu_custom_call" | custom-call | tf_op jit(solution)/shard_map/finish/pallas_call | solution.py:421

commit v7 on v6

--- a/solution.py
+++ b/solution.py
@@ -315,7 +315,7 @@
         part[1] = totals[1] - totals[0] * offset
 
     def start(mine, got, count, phase, targets):
-        along_x = count == XS
+        along_x = phase in (0, 2)
         base, here = (0 if phase in (0, 3) else count - 1), (x if along_x else z)
         for target in targets:
             @pl.when(here != target)

time: 26.5 us -> 26.5 us (level)
  no operation moved by 1% of the time
where the time goes in v7:
time: 26.5 us; the launch traced here: 26.2 us
  Pallas kernels  25.6 us (97%)
  between operations  0.64 us (2%)
    pallas_call x1, Pallas kernels, per_device(): pl.pallas_call(functools.partial(kernel, npy, npx), name='diffuse', out_s...  24.6 us
    pallas_call x1, Pallas kernels, per_device(): pl.pallas_call(finish, name='finish', out_shape=(shape, shape), in_specs=...  1 us

profile of v7, /device:TPU:8, one launch (start us, length us, event | category | flops | bytes accessed | tf_op | source)
XLA Modules:
  0.0 26.2 jit_solution(584043859985342866)
XLA Ops:
  0.6 24.6 %diffuse.1 = (f32[32,32,128]{2,1,0:T(8,128)S(1)}, f32[2,32,128]{2,1,0:T(8,128)S(1)}) custom-call(f32[32,32,128]{2,1,0:T(8,128)} %d_hbm.1, f32[32,32,128]{2,1,0:T(8,128)} %c_hbm.1, f32[32,32,128]{2,1,0:T(8,128)} %s_hbm.1), custom_call_target="tpu_custom_call" | custom-call | tf_op jit(solution)/shard_map/diffuse/pallas_call | solution.py:401
  25.2 1.0 %finish.1 = (f32[32,32,128]{2,1,0:T(8,128)}, f32[32,32,128]{2,1,0:T(8,128)}) custom-call(f32[32,32,128]{2,1,0:T(8,128)S(1)} %get-tuple-element.4.end, f32[2,32,128]{2,1,0:T(8,128)S(1)} %get-tuple-element.5.stats), custom_call_target="tpu_custom_call" | custom-call | tf_op jit(solution)/shard_map/finish/pallas_call | solution.py:421

commit v8 on v7

--- a/solution.py
+++ b/solution.py
@@ -47,10 +47,10 @@
 
     whole = same(LEFT, COLS)
     if a and b:
-        return [[
-            to(FIELD, rows_of(1, 2), cols_of(1, 5)), to(FIELD, rows_of(3, 5), cols_of(1, 3)),
-            to(COEF, rows_of(1, 2), cols_of(1, 4)), to(COEF, rows_of(3, 4), cols_of(1, 2)),
-        ]]
+        return [
+            [to(FIELD, rows_of(r, r), cols_of(1, STEPS - r)) for r in range(1, STEPS)]
+            + [to(COEF, rows_of(r, r), cols_of(1, STEPS - 1 - r)) for r in range(1, STEPS - 1)]
+        ]
     if b:
         return [[to(FIELD, same(TOP, ROWS), cols_of(1, STEPS)), to(COEF, same(TOP, ROWS), cols_of(1, STEPS - 1))]]
     edges = []
@@ -355,10 +355,21 @@
 
     with jax.named_scope("xa"):
         mid_part[0, 0], mid_part[0, 1] = collect(halves[0], xin, XS, 0, cells)
-    start(mid_part.at[0], zin, zs, 3, range(zs))
+    early = z < zs // 2
+    start(mid_part.at[0], zin, zs, 3, range(zs // 2))
+
+    @pl.when(jnp.logical_not(early))
+    def _():
+        start(mid_part.at[0], zin, zs, 3, range(zs // 2, zs))
+
     with jax.named_scope("zb"):
         mid_part[1, 0], mid_part[1, 1] = collect(halves[1], zin, zs, 1, cells)
     start(mid_part.at[1], xin, XS, 2, X_ORDER)
+
+    @pl.when(early)
+    def _():
+        start(mid_part.at[0], zin, zs, 3, range(zs // 2, zs))
+
     with jax.named_scope("za"):
         mean_a, spread_a = collect(mid_part.at[0], zin, zs, 3, cells * XS)
         stats[0, :HALF] = mean_a

time: 26.5 us -> 26.4 us (level)
  no operation moved by 1% of the time
where the time goes in v8:
time: 26.4 us; the launch traced here: 26 us
  Pallas kernels  25.4 us (96%)
  between operations  0.64 us (2%)
    pallas_call x1, Pallas kernels, per_device(): pl.pallas_call(functools.partial(kernel, npy, npx), name='diffuse', out_s...  24.4 us
    pallas_call x1, Pallas kernels, per_device(): pl.pallas_call(finish, name='finish', out_shape=(shape, shape), in_specs=...  1 us

profile of v8, /device:TPU:8, one launch (start us, length us, event | category | flops | bytes accessed | tf_op | source)
XLA Modules:
  0.0 26.0 jit_solution(1027792189926451210)
XLA Ops:
  0.6 24.4 %diffuse.1 = (f32[32,32,128]{2,1,0:T(8,128)S(1)}, f32[2,32,128]{2,1,0:T(8,128)S(1)}) custom-call(f32[32,32,128]{2,1,0:T(8,128)} %d_hbm.1, f32[32,32,128]{2,1,0:T(8,128)} %c_hbm.1, f32[32,32,128]{2,1,0:T(8,128)} %s_hbm.1), custom_call_target="tpu_custom_call" | custom-call | tf_op jit(solution)/shard_map/diffuse/pallas_call | solution.py:412
  25.0 1.0 %finish.1 = (f32[32,32,128]{2,1,0:T(8,128)}, f32[32,32,128]{2,1,0:T(8,128)}) custom-call(f32[32,32,128]{2,1,0:T(8,128)S(1)} %get-tuple-element.4.end, f32[2,32,128]{2,1,0:T(8,128)S(1)} %get-tuple-element.5.stats), custom_call_target="tpu_custom_call" | custom-call | tf_op jit(solution)/shard_map/finish/pallas_call | solution.py:432

commit v9 on v8

--- a/solution.py
+++ b/solution.py
@@ -14,8 +14,8 @@
 TOP, LEFT = STEPS, 8
 HIGH, WIDE = ROWS + 2 * STEPS, COLS + 2 * LEFT
 HALF = COLS // 2
-ROWS_OWN, ROWS_SIDE = 6, 6
-X_ORDER = (0, 1, 3, 2)
+ROWS_OWN, ROWS_SIDE = 10, 10
+X_ORDER = (0, 3, 1, 2)
 NEAR_FAR = ((0, 1), (2,))
 MESH = pl.DeviceIdType.MESH
 SIDES = [(a, b) for a in (-1, 0, 1) for b in (-1, 0, 1) if a or b]

time: 26.4 us -> 26.4 us (level)
  no operation moved by 1% of the time
where the time goes in v9:
time: 26.4 us; the launch traced here: 26 us
  Pallas kernels  25.4 us (96%)
  between operations  0.64 us (2%)
    pallas_call x1, Pallas kernels, per_device(): pl.pallas_call(functools.partial(kernel, npy, npx), name='diffuse', out_s...  24.4 us
    pallas_call x1, Pallas kernels, per_device(): pl.pallas_call(finish, name='finish', out_shape=(shape, shape), in_specs=...  1 us

profile of v9, /device:TPU:8, one launch (start us, length us, event | category | flops | bytes accessed | tf_op | source)
XLA Modules:
  0.0 26.0 jit_solution(12333161307688697658)
XLA Ops:
  0.6 24.4 %diffuse.1 = (f32[32,32,128]{2,1,0:T(8,128)S(1)}, f32[2,32,128]{2,1,0:T(8,128)S(1)}) custom-call(f32[32,32,128]{2,1,0:T(8,128)} %d_hbm.1, f32[32,32,128]{2,1,0:T(8,128)} %c_hbm.1, f32[32,32,128]{2,1,0:T(8,128)} %s_hbm.1), custom_call_target="tpu_custom_call" | custom-call | tf_op jit(solution)/shard_map/diffuse/pallas_call | solution.py:412
  25.0 1.0 %finish.1 = (f32[32,32,128]{2,1,0:T(8,128)}, f32[32,32,128]{2,1,0:T(8,128)}) custom-call(f32[32,32,128]{2,1,0:T(8,128)S(1)} %get-tuple-element.4.end, f32[2,32,128]{2,1,0:T(8,128)S(1)} %get-tuple-element.5.stats), custom_call_target="tpu_custom_call" | custom-call | tf_op jit(solution)/shard_map/finish/pallas_call | solution.py:432
